TPU v7x, 256 devices: a whole 4x4x8 slice. The times are simulated.
256 devices in a mesh: tm: 64 (over z, y, core), mp: 4 (over x).
Axes of the slice: x: 4, y: 4, z: 8, core: 2. Of those that a mesh axis runs over, the one named last changes fastest.
Arguments:
- latents: float32 [4, 64, 4, 4096], P(None, 'tm'), may hold values from -6 to 6
- noise: float32 [4, 64, 4, 4096], P(None, 'tm'), may hold values from -6 to 6
- start_step: int32 [4], replicated, may hold values from 64 to 999
- slide: int32 [4], replicated, may hold values from 1 to 64, as said below
- w_in: float32 [4, 320], replicated, may hold values from -3 to 3
- w_gate: bfloat16 [320, 1280], P(None, 'mp'), may hold values from -0.3125 to 0.3125
- w_value: bfloat16 [320, 1280], P(None, 'mp'), may hold values from -0.3125 to 0.3125
- w_down: bfloat16 [1280, 320], P('mp'), may hold values from -0.15625 to 0.15625
- w_out: float32 [320, 4], replicated, may hold values from -0.3125 to 0.3125
Outputs:
- next_window: float32 [4, 64, 4, 4096], P(None, 'tm')
- eps: float32 [4, 64, 4, 4096], P(None, 'tm', None, 'mp')
Inputs may be any that keep to these rules, and one draw needn't show every extreme that they name: `slide`: some prompt slides by exactly 64, and another by exactly 1.
All inputs are finite; a program needn't handle non-finite values.
Results may differ from a plain program's by a relative error of at most 0.0023.
Values sent between devices are 32-bit elements; how exact they have to be, the bound alone decides.
A program may use at most 64 MiB of HBM per device.

v0:
```python
import math

import jax
import jax.numpy as jnp
from jax import lax
from jax.sharding import Mesh
from jax.sharding import PartitionSpec as P

TSTEPS = 1000
TM = ("tm_0", "tm_1", "tm_2")


def cut_along(x, dim, peers):
    dims = x.shape
    parts = x.reshape(*dims[:dim], peers, dims[dim] // peers, *dims[dim + 1 :])
    return jnp.moveaxis(parts, dim, 0)


def summed_on_arrival(x, axis, dim):
    peers = lax.axis_size(axis)
    parts = lax.all_to_all(cut_along(x, dim, peers), axis, 0, 0, tiled=True)
    return jnp.sum(parts, axis=0)


def filled_with(x, identity):
    return jnp.zeros_like(x) + jnp.asarray(identity, x.dtype)


def entering(x, axes, combine, identity):
    before = start = filled_with(x, identity)
    total = x
    for axis in reversed(axes):
        peers, mine = (lax.axis_size(axis), lax.axis_index(axis))
        pieces = lax.all_gather(total, axis)
        inside, total = (start, start)
        for k in range(peers):
            passed = k < mine
            total = combine(total, pieces[k])
            inside = jnp.where(passed, total, inside)
        before = combine(inside, before)
    return before


def from_root(x, axis, root):
    return lax.dynamic_index_in_dim(lax.all_gather(x, axis), root, 0, keepdims=False)


def from_behind(block, axis, distance):
    devices = range(lax.axis_size(axis))
    route = [(i - distance, i) for i in devices if i - distance in devices]
    return lax.ppermute(block, axis, route)


def sent_to_all(x, axis):
    peers = lax.axis_size(axis)
    return lax.all_to_all(jnp.broadcast_to(x[None], (peers, *x.shape)), axis, 0, 0, tiled=True)


def in_order(parts, dim):
    parts = jnp.moveaxis(parts, 0, dim)
    dims = parts.shape
    return parts.reshape(*dims[:dim], dims[dim] * dims[dim + 1], *dims[dim + 2 :])


def gather_directly(x, axis, dim):
    parts = sent_to_all(x, axis)
    return in_order(parts, dim)


def plan(count):
    steps_f = jnp.arange(count, dtype=jnp.float32)
    beta = 0.0001 + (0.02 - 0.0001) * steps_f / (count - 1)
    abar = jnp.cumprod(1.0 - beta)
    return (beta, abar)


def lookup(table, times):
    grid = jnp.arange(table.shape[0], dtype=jnp.int32)
    return jnp.sum(jnp.where(times[..., None] == grid, table, 0.0), axis=-1)


def embed(times, channels):
    half = channels // 2
    freq = jnp.exp(-math.log(10000.0) * jnp.arange(half, dtype=jnp.float32) / half)
    angle = times[..., None] * freq
    return jnp.concatenate([jnp.cos(angle), jnp.sin(angle)], axis=-1)


def add_terms(earlier, later):
    return earlier + later


def shards(latents, noise, start_step, slide, w_in, w_gate, w_value, w_down, w_out):
    prompts, t_dev, lat, pos = latents.shape
    channels = w_in.shape[1]
    n_tm = lax.axis_size(TM)
    window = n_tm * t_dev
    share_width = pos // lax.axis_size("mp")
    share_offset = lax.axis_index("mp") * share_width
    slots = lax.axis_index(TM) * t_dev + jnp.arange(t_dev, dtype=jnp.int32)
    times = start_step[:, None] - slots[None, :]
    beta, abar = plan(TSTEPS)
    beta_t = lookup(beta, times)[:, :, None, None]
    abar_t = lookup(abar, times)[:, :, None, None]
    vectors = embed(times.astype(jnp.float32), channels).reshape(prompts * t_dev, channels)
    folded = jnp.dot(w_down.astype(jnp.float32), w_out, precision=lax.Precision.HIGHEST)
    items = latents.reshape(prompts * t_dev, lat, pos)

    def denoise(pair):
        latent, vector = pair
        hid = jnp.dot(w_in.T, latent, precision=lax.Precision.HIGHEST) + vector[:, None]
        mean = jnp.mean(hid, axis=0)
        var = jnp.mean((hid - mean) ** 2, axis=0)
        normed = ((hid - mean) * lax.rsqrt(var + 1e-05)).astype(jnp.bfloat16)
        gate = jnp.einsum("cf,cp->fp", w_gate, normed, preferred_element_type=jnp.float32)
        value = jnp.einsum("cf,cp->fp", w_value, normed, preferred_element_type=jnp.float32)
        hidden = (jax.nn.gelu(gate, approximate=False) * value).astype(jnp.bfloat16)
        partial_eps = jnp.dot(folded.T, hidden, precision=lax.Precision.HIGHEST)
        base_eps = jnp.dot(w_out.T, hid, precision=lax.Precision.HIGHEST)
        return (partial_eps, base_eps)

    partials, bases = lax.map(denoise, (items, vectors))
    summed = summed_on_arrival(partials, "mp", 2)
    eps = summed + lax.dynamic_slice_in_dim(bases, share_offset, share_width, 2)
    current = lax.dynamic_slice_in_dim(latents, share_offset, share_width, 3)
    sampled = lax.dynamic_slice_in_dim(noise, share_offset, share_width, 3)
    eps = eps.reshape(prompts, t_dev, lat, share_width)
    stepped = (current - beta_t / jnp.sqrt(1.0 - abar_t) * eps) / jnp.sqrt(1.0 - beta_t) + jnp.sqrt(
        beta_t
    ) * sampled
    drift = stepped - current
    first = (slots == 0)[None, :, None, None]
    head_part = jnp.where(first, current, 0.0)
    terms = drift + head_part
    totals = jnp.sum(terms, axis=1)
    before = entering(totals, TM, add_terms, jnp.zeros_like(totals))
    updated = before[:, None] + (jnp.cumsum(terms, axis=1) - terms) + head_part
    last = from_root(updated[:, -1], TM, n_tm - 1)
    moved = updated
    for bit in range((window // 2).bit_length()):
        step = 1 << bit
        incoming = from_behind(moved, TM, -max(1, step // t_dev))
        taken = slide >> bit & 1 == 1
        moved = jnp.where(taken[:, None, None, None], incoming, moved)
    beyond = slots[None, :] + slide[:, None] >= window
    result = jnp.where(beyond[:, :, None, None], last[:, None], moved)
    result = gather_directly(result, "mp", 3)
    return (result, eps)


def solution(mesh):
    split = Mesh(mesh.devices.reshape(8, 4, 2, mesh.shape["mp"]), ("tm_0", "tm_1", "tm_2", "mp"))
    in_specs = (
        P(None, TM, None, None),
        P(None, TM, None, None),
        P(),
        P(),
        P(),
        P(None, "mp"),
        P(None, "mp"),
        P("mp", None),
        P(),
    )
    out_specs = (P(None, TM, None, None), P(None, TM, None, "mp"))
    return jax.shard_map(
        shards, mesh=split, in_specs=in_specs, out_specs=out_specs, check_vma=False
    )
```

profile of v0, /device:TPU:1, one launch (start us, length us, event | category | flops | bytes accessed | tf_op | source)
XLA Modules:
  0.0 264.8 jit_solution(2865987861972973515)
XLA Ops:
  9.7 99.4 %while.12 = (s32[]{:T(128)}, f32[4,4,4096]{2,1,0:T(4,128)S(1)}, f32[4,4,4096]{2,1,0:T(4,128)S(1)}, f32[4,4,4096]{2,1,0:T(4,128)}, f32[4,320]{1,0:T(4,128)}, /*in...) while((s32[]{:T(128)}, f32[4,4,4096]{2,1,0:T(4,128)S(1)}, ...), condition=%wide.region_7.8_spmd, body=%wide.region_4.7_spmd.sunk | while | flops 1967394816 | bytes 44411340 | solution.py:122
  9.8 5.3 %fusion.70 = (f32[4096]{0:T(1024)S(1)}, f32[4096,320]{0,1:T(8,128)S(1)}) fusion(f32[320]{0:T(512)S(1)} %dynamic-slice_reduce_fusion.2, f32[4,320]{1,0:T(4,128)} %get-tuple-element.192, f32[4,4,4096]{2,1,0:T(4,128)} %get-tuple-element.191, s32[]{:T(128)} %get-tuple-element.177), kind=kOutput, calls=%fused_computation.101.clone.1 | convolution fusion | flops 65531904 | bytes 5332736 | tf_op jit(solution)/shard_map/while/body/eval_jaxpr/dot_general | solution.py:111
  17.4 13.1 %fusion.72 = bf16[320,4096]{1,0:T(8,128)(2,1)S(1)} fusion(bf16[320,320]{1,0:T(8,128)(2,1)S(1)} %copy-done.5, f32[4096,320]{0,1:T(8,128)S(1)} %fusion.71, f32[4096,320]{0,1:T(8,128)S(1)} %get-tuple-element.164, f32[4096]{0:T(1024)S(1)} %add_rsqrt_fusion.2, f32[4096]{0:T(1024)S(1)} %broadcast_multiply_fusion.2), kind=kOutput, calls=%fused_computation.4.clone.1 | convolution fusion | flops 929300480 | bytes 13344768 | tf_op jit(solution)/shard_map/while/body/eval_jaxpr/cf,cp->fp/dot_general | solution.py:116
  34.6 5.3 %fusion.70 = (f32[4096]{0:T(1024)S(1)}, f32[4096,320]{0,1:T(8,128)S(1)}) fusion(f32[320]{0:T(512)S(1)} %dynamic-slice_reduce_fusion.2, f32[4,320]{1,0:T(4,128)} %get-tuple-element.192, f32[4,4,4096]{2,1,0:T(4,128)} %get-tuple-element.191, s32[]{:T(128)} %get-tuple-element.177), kind=kOutput, calls=%fused_computation.101.clone.1 | convolution fusion | flops 65531904 | bytes 5332736 | tf_op jit(solution)/shard_map/while/body/eval_jaxpr/dot_general | solution.py:111
  42.2 13.1 %fusion.72 = bf16[320,4096]{1,0:T(8,128)(2,1)S(1)} fusion(bf16[320,320]{1,0:T(8,128)(2,1)S(1)} %copy-done.5, f32[4096,320]{0,1:T(8,128)S(1)} %fusion.71, f32[4096,320]{0,1:T(8,128)S(1)} %get-tuple-element.164, f32[4096]{0:T(1024)S(1)} %add_rsqrt_fusion.2, f32[4096]{0:T(1024)S(1)} %broadcast_multiply_fusion.2), kind=kOutput, calls=%fused_computation.4.clone.1 | convolution fusion | flops 929300480 | bytes 13344768 | tf_op jit(solution)/shard_map/while/body/eval_jaxpr/cf,cp->fp/dot_general | solution.py:116
  59.4 5.3 %fusion.70 = (f32[4096]{0:T(1024)S(1)}, f32[4096,320]{0,1:T(8,128)S(1)}) fusion(f32[320]{0:T(512)S(1)} %dynamic-slice_reduce_fusion.2, f32[4,320]{1,0:T(4,128)} %get-tuple-element.192, f32[4,4,4096]{2,1,0:T(4,128)} %get-tuple-element.191, s32[]{:T(128)} %get-tuple-element.177), kind=kOutput, calls=%fused_computation.101.clone.1 | convolution fusion | flops 65531904 | bytes 5332736 | tf_op jit(solution)/shard_map/while/body/eval_jaxpr/dot_general | solution.py:111
  67.0 13.1 %fusion.72 = bf16[320,4096]{1,0:T(8,128)(2,1)S(1)} fusion(bf16[320,320]{1,0:T(8,128)(2,1)S(1)} %copy-done.5, f32[4096,320]{0,1:T(8,128)S(1)} %fusion.71, f32[4096,320]{0,1:T(8,128)S(1)} %get-tuple-element.164, f32[4096]{0:T(1024)S(1)} %add_rsqrt_fusion.2, f32[4096]{0:T(1024)S(1)} %broadcast_multiply_fusion.2), kind=kOutput, calls=%fused_computation.4.clone.1 | convolution fusion | flops 929300480 | bytes 13344768 | tf_op jit(solution)/shard_map/while/body/eval_jaxpr/cf,cp->fp/dot_general | solution.py:116
  84.2 5.3 %fusion.70 = (f32[4096]{0:T(1024)S(1)}, f32[4096,320]{0,1:T(8,128)S(1)}) fusion(f32[320]{0:T(512)S(1)} %dynamic-slice_reduce_fusion.2, f32[4,320]{1,0:T(4,128)} %get-tuple-element.192, f32[4,4,4096]{2,1,0:T(4,128)} %get-tuple-element.191, s32[]{:T(128)} %get-tuple-element.177), kind=kOutput, calls=%fused_computation.101.clone.1 | convolution fusion | flops 65531904 | bytes 5332736 | tf_op jit(solution)/shard_map/while/body/eval_jaxpr/dot_general | solution.py:111
  91.8 13.1 %fusion.72 = bf16[320,4096]{1,0:T(8,128)(2,1)S(1)} fusion(bf16[320,320]{1,0:T(8,128)(2,1)S(1)} %copy-done.5, f32[4096,320]{0,1:T(8,128)S(1)} %fusion.71, f32[4096,320]{0,1:T(8,128)S(1)} %get-tuple-element.164, f32[4096]{0:T(1024)S(1)} %add_rsqrt_fusion.2, f32[4096]{0:T(1024)S(1)} %broadcast_multiply_fusion.2), kind=kOutput, calls=%fused_computation.4.clone.1 | convolution fusion | flops 929300480 | bytes 13344768 | tf_op jit(solution)/shard_map/while/body/eval_jaxpr/cf,cp->fp/dot_general | solution.py:116
  110.2 4.8 %all-to-all-start = ((f32[4,4,4,1024]{3,2,1,0:T(4,128)}), f32[4,4,4,1024]{3,2,1,0:T(4,128)S(1)}, u32[]{:S(2)}, u32[]{:S(2)}) async-start(f32[4,4,4,1024]{3,2,1,0:T(4,128)} %copy.44), calls=%async_computation | async-start | bytes 524288 | tf_op jit(solution)/shard_map/all_to_all | solution.py:21
  115.9 4.7 %all-to-all-done = f32[4,4,4,1024]{3,2,1,0:T(4,128)S(1)} async-done(((f32[4,4,4,1024]{3,2,1,0:T(4,128)}), f32[4,4,4,1024]{3,2,1,0:T(4,128)S(1)}, u32[]{:S(2)}, u32[]{:S(2)}) %all-to-all-start) | async-done | bytes 262176 | tf_op jit(solution)/shard_map/all_to_all | solution.py:21
  121.6 4.4 %all-gather = f32[8,1,4,1024]{3,2,1,0:T(4,128)S(1)} all-gather(f32[4,1,4,1024]{3,2,1,0:T(4,128)S(1)} %fusion.26), channel_id=2, replica_groups=mesh['tm_0'=8,'tm_1'=4,'tm_2'=2,'mp'=4] {'tm_2'}, dimensions={0}, use_global_device_ids=true | all-gather | bytes 196608 | tf_op jit(solution)/shard_map/all_gather | solution.py:34
  126.1 9.9 %all-gather.2 = f32[16,1,4,1024]{3,2,1,0:T(4,128)S(1)} all-gather(f32[4,1,4,1024]{3,2,1,0:T(4,128)S(1)} %fusion.38), channel_id=4, replica_groups=mesh['tm_0'=8,'tm_1'=4,'tm_2'=2,'mp'=4] {'tm_1'}, dimensions={0}, use_global_device_ids=true | all-gather | bytes 327680 | tf_op jit(solution)/shard_map/all_gather | solution.py:34
  136.0 22.5 %all_gather.20 = f32[8,4,4,1024]{3,2,1,0:T(4,128)S(1)} all-gather(f32[1,4,4,1024]{3,2,1,0:T(4,128)S(1)} %fusion.33), channel_id=1, replica_groups=mesh['tm_0'=8,'tm_1'=4,'tm_2'=2,'mp'=4] {'tm_0'}, dimensions={0}, use_global_device_ids=true | all-gather | bytes 589824 | tf_op jit(solution)/shard_map/all_gather | solution.py:34
  160.2 10.8 %collective-permute-start = (f32[4,1,4,1024]{3,2,1,0:T(4,128)}, f32[4,1,4,1024]{3,2,1,0:T(4,128)S(1)}, u32[]{:S(2)}, u32[]{:S(2)}) collective-permute-start(f32[4,1,4,1024]{3,2,1,0:T(4,128)} %fusion.32), channel_id=1, source_target_pairs={{4,0},{8,4},{12,8},{16,12},{20,16},{24,20},{28,24},{32,28},{36,32}... | collective-permute-start | bytes 196616 | tf_op jit(solution)/shard_map/ppermute | solution.py:51
  171.1 3.4 %collective-permute-done = f32[4,1,4,1024]{3,2,1,0:T(4,128)S(1)} collective-permute-done((f32[4,1,4,1024]{3,2,1,0:T(4,128)}, f32[4,1,4,1024]{3,2,1,0:T(4,128)S(1)}, u32[]{:S(2)}, u32[]{:S(2)}) %collective-permute-start) | collective-permute-done | bytes 65568 | tf_op jit(solution)/shard_map/ppermute | solution.py:51
  176.7 3.7 %collective-permute-done.1 = f32[4,1,4,1024]{3,2,1,0:T(4,128)S(1)} collective-permute-done((f32[4,1,4,1024]{3,2,1,0:T(4,128)S(1)}, f32[4,1,4,1024]{3,2,1,0:T(4,128)S(1)}, u32[]{:S(2)}, u32[]{:S(2)}) %collective-permute-start.1) | collective-permute-done | bytes 65568 | tf_op jit(solution)/shard_map/ppermute | solution.py:51
  181.8 6.3 %collective-permute-done.2 = f32[4,1,4,1024]{3,2,1,0:T(4,128)S(1)} collective-permute-done((f32[4,1,4,1024]{3,2,1,0:T(4,128)S(1)}, f32[4,1,4,1024]{3,2,1,0:T(4,128)S(1)}, u32[]{:S(2)}, u32[]{:S(2)}) %collective-permute-start.2) | collective-permute-done | bytes 65568 | tf_op jit(solution)/shard_map/ppermute | solution.py:51
  189.5 3.7 %collective-permute-done.3 = f32[4,1,4,1024]{3,2,1,0:T(4,128)S(1)} collective-permute-done((f32[4,1,4,1024]{3,2,1,0:T(4,128)S(1)}, f32[4,1,4,1024]{3,2,1,0:T(4,128)S(1)}, u32[]{:S(2)}, u32[]{:S(2)}) %collective-permute-start.3) | collective-permute-done | bytes 65568 | tf_op jit(solution)/shard_map/ppermute | solution.py:51
  194.6 4.7 %collective-permute-done.4 = f32[4,1,4,1024]{3,2,1,0:T(4,128)S(1)} collective-permute-done((f32[4,1,4,1024]{3,2,1,0:T(4,128)S(1)}, f32[4,1,4,1024]{3,2,1,0:T(4,128)S(1)}, u32[]{:S(2)}, u32[]{:S(2)}) %collective-permute-start.4) | collective-permute-done | bytes 65568 | tf_op jit(solution)/shard_map/ppermute | solution.py:51
  200.7 7.6 %collective-permute-done.5 = f32[4,1,4,1024]{3,2,1,0:T(4,128)S(1)} collective-permute-done((f32[4,1,4,1024]{3,2,1,0:T(4,128)S(1)}, f32[4,1,4,1024]{3,2,1,0:T(4,128)S(1)}, u32[]{:S(2)}, u32[]{:S(2)}) %collective-permute-start.5) | collective-permute-done | bytes 65568 | tf_op jit(solution)/shard_map/ppermute | solution.py:51
  208.3 37.4 %all-gather.5.cloned.1.call-done = f32[256,1,4,1024]{3,2,1,0:T(4,128)} async-done(((f32[4,1,4,1024]{3,2,1,0:T(4,128)}), f32[256,1,4,1024]{3,2,1,0:T(4,128)}) %all-gather.5.cloned.1.call-update) | async-done | bytes 4194320 | tf_op jit(solution)/shard_map/all_gather | solution.py:45
  247.4 4.0 %all-to-all-start.1 = ((f32[4,4,1,4,1024]{4,3,1,2,0:T(4,128)}), f32[4,4,1,4,1024]{4,3,1,2,0:T(4,128)S(1)}, u32[]{:S(2)}, u32[]{:S(2)}) async-start(f32[4,4,1,4,1024]{4,3,1,2,0:T(4,128)} %broadcast_in_dim.121), calls=%async_computation.1 | async-start | bytes 524288 | tf_op jit(solution)/shard_map/all_to_all | solution.py:56
  252.0 5.3 %all-to-all-done.1 = f32[4,4,1,4,1024]{4,3,1,2,0:T(4,128)S(1)} async-done(((f32[4,4,1,4,1024]{4,3,1,2,0:T(4,128)}), f32[4,4,1,4,1024]{4,3,1,2,0:T(4,128)S(1)}, u32[]{:S(2)}, u32[]{:S(2)}) %all-to-all-start.1) | async-done | bytes 262176 | tf_op jit(solution)/shard_map/all_to_all | solution.py:56
  (99 shorter events, 42.9 us)
Async XLA Ops:
  7.2 1.6 copy-start
  9.7 106.0 %copy-start.3 = (s32[4]{0:T(128)S(1)}, s32[4]{0:T(128)}, u32[]{:S(2)}) copy-start(s32[4]{0:T(128)} %get-tuple-element.86) | copy-start | bytes 52
  9.7 161.4 %copy-start.4 = (s32[4]{0:T(128)S(1)}, s32[4]{0:T(128)}, u32[]{:S(2)}) copy-start(s32[4]{0:T(128)} %param.14) | copy-start | bytes 52
  9.8 6.0 %copy-start.1 = (bf16[320,320]{1,0:T(8,128)(2,1)S(1)}, bf16[320,320]{1,0:T(8,128)(2,1)}, u32[]{:S(2)}) copy-start(bf16[320,320]{1,0:T(8,128)(2,1)} %get-tuple-element.194) | copy-start | bytes 614404 | tf_op jit(solution)/shard_map/while
  15.8 1.6 copy-start.5
  17.4 14.3 %copy-start.2 = (f32[320,4]{0,1:T(4,128)S(1)}, f32[320,4]{0,1:T(4,128)}, u32[]{:S(2)}) copy-start(f32[320,4]{0,1:T(4,128)} %get-tuple-element.197) | copy-start | bytes 15364 | tf_op jit(solution)/shard_map/while
  34.6 6.0 %copy-start.1 = (bf16[320,320]{1,0:T(8,128)(2,1)S(1)}, bf16[320,320]{1,0:T(8,128)(2,1)}, u32[]{:S(2)}) copy-start(bf16[320,320]{1,0:T(8,128)(2,1)} %get-tuple-element.194) | copy-start | bytes 614404 | tf_op jit(solution)/shard_map/while
  40.6 1.6 copy-start.5
  42.2 14.3 %copy-start.2 = (f32[320,4]{0,1:T(4,128)S(1)}, f32[320,4]{0,1:T(4,128)}, u32[]{:S(2)}) copy-start(f32[320,4]{0,1:T(4,128)} %get-tuple-element.197) | copy-start | bytes 15364 | tf_op jit(solution)/shard_map/while
  59.4 6.0 %copy-start.1 = (bf16[320,320]{1,0:T(8,128)(2,1)S(1)}, bf16[320,320]{1,0:T(8,128)(2,1)}, u32[]{:S(2)}) copy-start(bf16[320,320]{1,0:T(8,128)(2,1)} %get-tuple-element.194) | copy-start | bytes 614404 | tf_op jit(solution)/shard_map/while
  65.4 1.6 copy-start.5
  67.0 14.3 %copy-start.2 = (f32[320,4]{0,1:T(4,128)S(1)}, f32[320,4]{0,1:T(4,128)}, u32[]{:S(2)}) copy-start(f32[320,4]{0,1:T(4,128)} %get-tuple-element.197) | copy-start | bytes 15364 | tf_op jit(solution)/shard_map/while
  84.2 6.0 %copy-start.1 = (bf16[320,320]{1,0:T(8,128)(2,1)S(1)}, bf16[320,320]{1,0:T(8,128)(2,1)}, u32[]{:S(2)}) copy-start(bf16[320,320]{1,0:T(8,128)(2,1)} %get-tuple-element.194) | copy-start | bytes 614404 | tf_op jit(solution)/shard_map/while
  90.2 1.6 copy-start.5
  91.8 14.3 %copy-start.2 = (f32[320,4]{0,1:T(4,128)S(1)}, f32[320,4]{0,1:T(4,128)}, u32[]{:S(2)}) copy-start(f32[320,4]{0,1:T(4,128)} %get-tuple-element.197) | copy-start | bytes 15364 | tf_op jit(solution)/shard_map/while
  110.2 10.3 %all-to-all-start = ((f32[4,4,4,1024]{3,2,1,0:T(4,128)}), f32[4,4,4,1024]{3,2,1,0:T(4,128)S(1)}, u32[]{:S(2)}, u32[]{:S(2)}) async-start(f32[4,4,4,1024]{3,2,1,0:T(4,128)} %copy.44), calls=%async_computation | async-start | bytes 524288 | tf_op jit(solution)/shard_map/all_to_all | solution.py:21
  115.1 130.7 %all-gather.5.cloned.1.call-start = ((), (), s32[]{:S(2)}) async-start(), calls=%async_computation.2 | async-start | bytes 4259840 | tf_op jit(solution)/shard_map/all_gather | solution.py:45
  160.2 14.3 %collective-permute-start = (f32[4,1,4,1024]{3,2,1,0:T(4,128)}, f32[4,1,4,1024]{3,2,1,0:T(4,128)S(1)}, u32[]{:S(2)}, u32[]{:S(2)}) collective-permute-start(f32[4,1,4,1024]{3,2,1,0:T(4,128)} %fusion.32), channel_id=1, source_target_pairs={{4,0},{8,4},{12,8},{16,12},{20,16},{24,20},{28,24},{32,28},{36,32}... | collective-permute-start | bytes 196616 | tf_op jit(solution)/shard_map/ppermute | solution.py:51
  175.4 5.0 %collective-permute-start.1 = (f32[4,1,4,1024]{3,2,1,0:T(4,128)S(1)}, f32[4,1,4,1024]{3,2,1,0:T(4,128)S(1)}, u32[]{:S(2)}, u32[]{:S(2)}) collective-permute-start(f32[4,1,4,1024]{3,2,1,0:T(4,128)S(1)} %broadcast_select_fusion), channel_id=1, source_target_pairs={{8,0},{12,4},{16,8},{20,12},{24,16},{28,20},{32,24},{36,28},{40,32... | collective-permute-start | bytes 196616 | tf_op jit(solution)/shard_map/ppermute | solution.py:51
  180.5 7.6 %collective-permute-start.2 = (f32[4,1,4,1024]{3,2,1,0:T(4,128)S(1)}, f32[4,1,4,1024]{3,2,1,0:T(4,128)S(1)}, u32[]{:S(2)}, u32[]{:S(2)}) collective-permute-start(f32[4,1,4,1024]{3,2,1,0:T(4,128)S(1)} %broadcast_select_fusion.1), channel_id=1, source_target_pairs={{16,0},{20,4},{24,8},{28,12},{32,16},{36,20},{40,24},{44,28},{48,3... | collective-permute-start | bytes 196616 | tf_op jit(solution)/shard_map/ppermute | solution.py:51
  188.2 5.0 %collective-permute-start.3 = (f32[4,1,4,1024]{3,2,1,0:T(4,128)S(1)}, f32[4,1,4,1024]{3,2,1,0:T(4,128)S(1)}, u32[]{:S(2)}, u32[]{:S(2)}) collective-permute-start(f32[4,1,4,1024]{3,2,1,0:T(4,128)S(1)} %broadcast_select_fusion.2), channel_id=1, source_target_pairs={{32,0},{36,4},{40,8},{44,12},{48,16},{52,20},{56,24},{60,28},{64,3... | collective-permute-start | bytes 196616 | tf_op jit(solution)/shard_map/ppermute | solution.py:51
  193.3 6.0 %collective-permute-start.4 = (f32[4,1,4,1024]{3,2,1,0:T(4,128)S(1)}, f32[4,1,4,1024]{3,2,1,0:T(4,128)S(1)}, u32[]{:S(2)}, u32[]{:S(2)}) collective-permute-start(f32[4,1,4,1024]{3,2,1,0:T(4,128)S(1)} %broadcast_select_fusion.3), channel_id=1, source_target_pairs={{64,0},{68,4},{72,8},{76,12},{80,16},{84,20},{88,24},{92,28},{96,3... | collective-permute-start | bytes 196616 | tf_op jit(solution)/shard_map/ppermute | solution.py:51
  199.4 8.9 %collective-permute-start.5 = (f32[4,1,4,1024]{3,2,1,0:T(4,128)S(1)}, f32[4,1,4,1024]{3,2,1,0:T(4,128)S(1)}, u32[]{:S(2)}, u32[]{:S(2)}) collective-permute-start(f32[4,1,4,1024]{3,2,1,0:T(4,128)S(1)} %broadcast_select_fusion.4), channel_id=1, source_target_pairs={{128,0},{132,4},{136,8},{140,12},{144,16},{148,20},{152,24},{156,2... | collective-permute-start | bytes 196616 | tf_op jit(solution)/shard_map/ppermute | solution.py:51
  247.4 9.9 %all-to-all-start.1 = ((f32[4,4,1,4,1024]{4,3,1,2,0:T(4,128)}), f32[4,4,1,4,1024]{4,3,1,2,0:T(4,128)S(1)}, u32[]{:S(2)}, u32[]{:S(2)}) async-start(f32[4,4,1,4,1024]{4,3,1,2,0:T(4,128)} %broadcast_in_dim.121), calls=%async_computation.1 | async-start | bytes 524288 | tf_op jit(solution)/shard_map/all_to_all | solution.py:56
Sparse Core Ops, SparseCore 0:
  160.4 85.3 all-gather.4
where the time goes:
time: 266 us; the launch traced here: 265 us
  matrix products  97.1 us (37%)
  waiting for transfers between devices  76.8 us (29%)
  blocking collectives  36.8 us (14%)
  starting transfers between devices  26.1 us (10%)
  between operations  14.3 us (5%)
  other arithmetic  10.2 us (4%)
  local copies, waits for them, and re-layouts  2.96 us (1%)
    dot_general x4, matrix products, denoise(): jnp.einsum('cf,cp->fp', w_value, normed, preferred_element_type=jnp.float32)  52.5 us
    all_gather x1, waiting for transfers between devices, from_root(): lax.all_gather(x, axis)  37.4 us
    all_gather x3, blocking collectives, entering(): pieces = lax.all_gather(total, axis)  36.8 us
    ppermute x6, waiting for transfers between devices, from_behind(): return lax.ppermute(block, axis, route)  29.4 us
    dot_general x4, matrix products, denoise(): jnp.dot(w_in.T, latent, precision=lax.Precision.HIGHEST) + vector[:, None]  21.3 us
    ppermute x6, starting transfers between devices, from_behind(): return lax.ppermute(block, axis, route)  17.3 us
    dot_general x4, matrix products, denoise(): base_eps = jnp.dot(w_out.T, hid, precision=lax.Precision.HIGHEST)  11.3 us
    dot_general x4, matrix products, denoise(): jnp.einsum('cf,cp->fp', w_gate, normed, preferred_element_type=jnp.float32)  6.42 us
  transfers between devices with their start and end apart: 9, of which 9 were waited for; matrix products, arithmetic and copies ran while one was open for 1% of the time, Pallas kernels for 0%

commit v1 on v0

v1 whole, which is shorter than its diff:
```python
import functools
import math

import jax
import jax.numpy as jnp
from jax import lax
from jax.experimental import pallas as pl
from jax.experimental.pallas import tpu as pltpu
from jax.sharding import PartitionSpec as P

TSTEPS = 1000
TILE = 512
SLOTS = 64
HIGHEST = lax.Precision.HIGHEST
MESH = pl.DeviceIdType.MESH


def split3(x):
    high = x.astype(jnp.bfloat16).astype(jnp.float32)
    rest = x - high
    mid = rest.astype(jnp.bfloat16).astype(jnp.float32)
    return high, mid, rest - mid


def contract_last(a, b):
    return lax.dot_general(
        a, b, (((1,), (1,)), ((), ())), precision=HIGHEST, preferred_element_type=jnp.float32
    )


def product_all(x):
    for axis, extent in ((1, 128), (0, 8)):
        step = 1
        while step < extent:
            x = x * pltpu.roll(x, step, axis)
            step *= 2
    return x


def scanner_of(prompt, lat):
    return (2 * lat + prompt % 2) * 8 + 2 * prompt + 1


def sweep(
    start, slide, lat_ref, noise_ref, w_in_ref, w_gate_ref, w_value_ref, w_down_ref, w_out_ref,
    out_ref, eps_ref,
    lhs, down, base_row, gram, coef, part, part_in, drift, slots_in, sums, picked, whole,
    part_send, part_recv, one_send, one_recv, two_send, two_recv, all_send, all_recv,
):
    prompts, _, lats, pos = lat_ref.shape
    channels = w_in_ref.shape[1]
    hidden = w_gate_ref.shape[1]
    share = pos // 4
    i = lax.axis_index("tm")
    m = lax.axis_index("mp")

    barrier = pltpu.get_barrier_semaphore()

    def greet(k, carry):
        pl.semaphore_signal(
            barrier, inc=1, device_id={"tm": lax.rem(i + k, SLOTS), "mp": m}, device_id_type=MESH
        )
        return carry

    for k in (1, 2, 3):
        pl.semaphore_signal(
            barrier, inc=1, device_id={"tm": i, "mp": lax.rem(m + k, 4)}, device_id_type=MESH
        )
    lax.fori_loop(1, SLOTS, greet, 0)

    row8 = lax.broadcasted_iota(jnp.int32, (8, channels), 0)
    lane8 = lax.broadcasted_iota(jnp.int32, (8, channels), 1)
    half = channels // 2
    steps = jnp.zeros((8, channels), jnp.int32)
    for p in range(prompts):
        steps = jnp.where(row8 == 4 + p, start[p] - i, steps)
    freq = jnp.exp(
        -math.log(10000.0) * jnp.where(lane8 < half, lane8, lane8 - half).astype(jnp.float32) / half
    )
    angle = steps.astype(jnp.float32) * freq
    emb = jnp.where(lane8 < half, jnp.cos(angle), jnp.sin(angle))
    w_in = w_in_ref[...]
    rows = jnp.where(row8 < 4, jnp.concatenate([w_in, w_in], axis=0), emb)
    centred = rows - jnp.mean(rows, axis=1, keepdims=True)
    gram[...] = contract_last(centred, centred) * (1.0 / channels)

    w_out = jnp.concatenate(
        [w_out_ref[...], jnp.zeros((channels, 124), jnp.float32)], axis=1
    )
    w_out_t = jnp.transpose(w_out)[:8, :]
    base_row[...] = contract_last(w_out_t, rows)

    def three_rows(x):
        return jnp.concatenate(split3(x) + (jnp.zeros_like(x),), axis=0).astype(jnp.bfloat16)

    lefts = three_rows(centred)
    tables = []
    for w_ref in (w_gate_ref, w_value_ref):
        pieces = jnp.dot(lefts, w_ref[...], preferred_element_type=jnp.float32)
        tables.append((pieces[0:8] + pieces[8:16] + pieces[16:24]) * math.sqrt(0.5))
    pieces = lax.dot_general(
        three_rows(w_out_t), w_down_ref[...], (((1,), (1,)), ((), ())),
        preferred_element_type=jnp.float32,
    )
    folded = pieces[0:8] + pieces[8:16] + pieces[16:24]
    high, mid, low = split3(folded)
    down[...] = jnp.concatenate([high, mid, low, jnp.zeros_like(low)], axis=0).astype(jnp.bfloat16)

    rowk = lax.broadcasted_iota(jnp.int32, (8, hidden), 0)
    for p in range(prompts):
        for q, table in enumerate(tables):
            own = jnp.where(
                rowk < 4, table, jnp.where(rowk == 4, table[4 + p : 5 + p, :], 0.0)
            )
            high, mid, low = split3(own)
            stack = jnp.concatenate(
                [high, high, mid, mid, high, low, jnp.zeros((80, hidden), jnp.float32)], axis=0
            )
            lhs[p, q * hidden : (q + 1) * hidden, :] = jnp.transpose(stack).astype(jnp.bfloat16)

    grid = (
        lax.broadcasted_iota(jnp.int32, (8, 128), 0) * 128
        + lax.broadcasted_iota(jnp.int32, (8, 128), 1)
    )

    def beta_at(k):
        return 0.0001 + (0.02 - 0.0001) * k.astype(jnp.float32) / (TSTEPS - 1)

    kept = 1.0 - beta_at(grid)
    for p in range(prompts):
        t = jnp.full((8, 128), start[p] - i, jnp.int32)
        abar = product_all(jnp.where(grid <= t, kept, 1.0))
        beta = beta_at(t)
        coef[p, 0] = beta / jnp.sqrt(1.0 - abar)
        coef[p, 1] = 1.0 / jnp.sqrt(1.0 - beta)
        coef[p, 2] = jnp.sqrt(beta)

    rowt = lax.broadcasted_iota(jnp.int32, (8, TILE), 0)

    def denoise(p):
        cov = gram[...]
        left = lhs[p]
        inner = down[...]

        def tile(n, carry):
            off = pl.multiple_of(n * TILE, TILE)
            x4 = lat_ref[p, 0, :, pl.ds(off, TILE)]
            x8 = jnp.concatenate([x4, x4], axis=0)
            x = jnp.where(rowt < 4, x8, 0.0)
            z = jnp.zeros((8, TILE), jnp.float32) + 2.0 * cov[:, 4 + p : 5 + p]
            for b in range(4):
                z = z + cov[:, b : b + 1] * x4[b : b + 1, :]
            var = jnp.sum(x * z, axis=0, keepdims=True) + cov[4 + p : 5 + p, 4 + p : 5 + p]
            scale = lax.rsqrt(var + 1e-05)
            y = jnp.where(rowt < 4, x8, jnp.where(rowt == 4, 1.0, 0.0)) * scale
            high, mid, low = split3(y)
            right = jnp.concatenate(
                [high, mid, high, mid, low, high, jnp.zeros((80, TILE), jnp.float32)], axis=0
            ).astype(jnp.bfloat16)
            both = jnp.dot(left, right, preferred_element_type=jnp.float32)
            g = both[:hidden]
            v = both[hidden:]
            act = (g * v * (1.0 + lax.erf(g))).astype(jnp.bfloat16)
            got = jnp.dot(inner, act, preferred_element_type=jnp.float32)
            got = got[0:8] + got[8:16] + got[16:24]
            per = share // TILE
            part[p, n // per, :, pl.ds(pl.multiple_of(lax.rem(n, per) * TILE, TILE), TILE)] = got[0:4]
            return carry

        lax.fori_loop(0, pos // TILE, tile, 0)

    def send_parts(p):
        for k in (1, 2, 3):
            peer = lax.rem(m + k, 4)
            pltpu.make_async_remote_copy(
                src_ref=part.at[p, peer], dst_ref=part_in.at[p, k - 1],
                send_sem=part_send, recv_sem=part_recv.at[p],
                device_id={"tm": i, "mp": peer}, device_id_type=MESH,
            ).start()

    def finish(p):
        pltpu.make_async_copy(part_in.at[p], part_in.at[p], part_recv.at[p]).wait()
        total = part[p, m] + part_in[p, 0] + part_in[p, 1] + part_in[p, 2]
        mine = pl.ds(pl.multiple_of(m * share, share), share)
        cur = lat_ref[p, 0, :, mine]
        nz = noise_ref[p, 0, :, mine]
        for a in range(4):
            total = total + base_row[0:4, a : a + 1] * cur[a : a + 1, :]
        total = total + base_row[0:4, 4 + p : 5 + p]
        eps_ref[p, 0] = total
        c1 = coef[p, 0][0:4]
        c2 = coef[p, 1][0:4]
        c3 = coef[p, 2][0:4]
        head = jnp.where(jnp.full((4, 128), i, jnp.int32) == 0, 1.0, 0.0)
        for s in range(8):
            lanes = slice(s * 128, (s + 1) * 128)
            term = (cur[:, lanes] - c1 * total[:, lanes]) * c2 + c3 * nz[:, lanes] - cur[:, lanes]
            drift[p, :, s, :] = term + head * cur[:, lanes]
        for a in range(lats):
            target = scanner_of(p, a)

            @pl.when(i != target)
            def _():
                pltpu.make_async_remote_copy(
                    src_ref=drift.at[p, a], dst_ref=slots_in.at[i],
                    send_sem=one_send, recv_sem=one_recv,
                    device_id={"tm": target, "mp": m}, device_id_type=MESH,
                ).start()

            @pl.when(i == target)
            def _():
                slots_in[SLOTS] = drift[p, a]

    pl_core = lax.rem(i, 2)
    my_prompt = lax.rem(i // 2, 4)
    my_z = i // 8
    my_lat = my_z // 2
    scanning = jnp.logical_and(pl_core == 1, lax.rem(my_z, 2) == lax.rem(my_prompt, 2))

    denoise(0)
    pl.semaphore_wait(barrier, SLOTS - 1 + 3)
    send_parts(0)
    for p in range(1, prompts):
        denoise(p)
        send_parts(p)
        finish(p - 1)
    finish(prompts - 1)

    @pl.when(scanning)
    def _():
        pltpu.make_async_copy(
            slots_in.at[pl.ds(0, SLOTS - 1)], slots_in.at[pl.ds(0, SLOTS - 1)], one_recv
        ).wait()
        slots_in[i] = slots_in[SLOTS]
        acc = slots_in[0]
        sums[1] = acc
        for j in range(1, SLOTS - 1):
            acc = acc + slots_in[j]
            sums[j + 1] = acc
        by = slide[my_prompt]
        for j in range(SLOTS):
            picked[j] = sums[jnp.minimum(j + by, SLOTS - 1)]

        def deliver(k, carry):
            peer = lax.rem(i + k, SLOTS)
            pltpu.make_async_remote_copy(
                src_ref=picked.at[peer], dst_ref=whole.at[my_prompt, m, my_lat],
                send_sem=two_send, recv_sem=two_recv.at[my_prompt],
                device_id={"tm": peer, "mp": m}, device_id_type=MESH,
            ).start()
            return carry

        lax.fori_loop(1, SLOTS, deliver, 0)
        whole[my_prompt, m, my_lat] = picked[i]

    for p in range(prompts):
        mine = jnp.logical_and(scanning, my_prompt == p)

        @pl.when(mine)
        def _():
            pltpu.make_async_copy(
                whole.at[p, m, pl.ds(0, lats - 1)], whole.at[p, m, pl.ds(0, lats - 1)], two_recv.at[p]
            ).wait()

        @pl.when(jnp.logical_not(mine))
        def _():
            pltpu.make_async_copy(whole.at[p, m], whole.at[p, m], two_recv.at[p]).wait()

        for k in (1, 2, 3):
            peer = lax.rem(m + k, 4)
            pltpu.make_async_remote_copy(
                src_ref=whole.at[p, m], dst_ref=whole.at[p, m],
                send_sem=all_send, recv_sem=all_recv.at[p],
                device_id={"tm": i, "mp": peer}, device_id_type=MESH,
            ).start()

    for p in range(prompts):
        pltpu.make_async_copy(
            whole.at[p, pl.ds(0, 3)], whole.at[p, pl.ds(0, 3)], all_recv.at[p]
        ).wait()
        for q in range(4):
            for s in range(8):
                out_ref[p, 0, :, q * share + s * 128 : q * share + (s + 1) * 128] = whole[p, q, :, s, :]

    def settle(ref, sem):
        pltpu.make_async_copy(ref, ref, sem).wait()

    settle(part_in, part_send)
    settle(whole.at[:, pl.ds(0, 3)], all_send)

    @pl.when(scanning)
    def _():
        settle(slots_in.at[pl.ds(0, SLOTS - 1)], two_send)
        settle(slots_in.at[pl.ds(0, prompts * lats - 1)], one_send)

    @pl.when(jnp.logical_not(scanning))
    def _():
        settle(slots_in.at[pl.ds(0, prompts * lats)], one_send)


def shards(latents, noise, start_step, slide, w_in, w_gate, w_value, w_down, w_out):
    prompts, _, lats, pos = latents.shape
    hidden = w_gate.shape[1]
    share = pos // 4
    f32 = jnp.float32
    smem = pl.BlockSpec(memory_space=pltpu.SMEM)
    vmem = pl.BlockSpec(memory_space=pltpu.VMEM)
    dma = pltpu.SemaphoreType.DMA
    return pl.pallas_call(
        sweep,
        out_shape=(
            jax.ShapeDtypeStruct(latents.shape, f32),
            jax.ShapeDtypeStruct((prompts, 1, lats, share), f32),
        ),
        in_specs=[smem, smem] + [vmem] * 7,
        out_specs=(vmem, vmem),
        scratch_shapes=[
            pltpu.VMEM((prompts, 2 * hidden, 128), jnp.bfloat16),
            pltpu.VMEM((32, hidden), jnp.bfloat16),
            pltpu.VMEM((8, 8), f32),
            pltpu.VMEM((8, 8), f32),
            pltpu.VMEM((prompts, 3, 8, 128), f32),
            pltpu.VMEM((prompts, 4, lats, share), f32),
            pltpu.VMEM((prompts, 3, lats, share), f32),
            pltpu.VMEM((prompts, lats, 8, 128), f32),
            pltpu.VMEM((SLOTS + 1, 8, 128), f32),
            pltpu.VMEM((SLOTS, 8, 128), f32),
            pltpu.VMEM((SLOTS, 8, 128), f32),
            pltpu.VMEM((prompts, 4, lats, 8, 128), f32),
            dma, dma((prompts,)), dma, dma, dma, dma((prompts,)), dma, dma((prompts,)),
        ],
        compiler_params=pltpu.CompilerParams(collective_id=0, has_side_effects=True),
        name="sweep",
    )(start_step, slide, latents, noise, w_in, w_gate, w_value, w_down, w_out)


def solution(mesh):
    in_specs = (
        P(None, "tm", None, None),
        P(None, "tm", None, None),
        P(),
        P(),
        P(),
        P(None, "mp"),
        P(None, "mp"),
        P("mp", None),
        P(),
    )
    out_specs = (P(None, "tm", None, None), P(None, "tm", None, "mp"))
    return jax.shard_map(shards, mesh=mesh, in_specs=in_specs, out_specs=out_specs, check_vma=False)
```

time: 266 us -> 52 us (0.20)
  matrix products: 97.1 us -> 0 us
  waiting for transfers between devices: 76.8 us -> 0 us
  Pallas kernels: 0 us -> 47.3 us
  blocking collectives: 36.8 us -> 0 us
  starting transfers between devices: 26.1 us -> 0 us
  between operations: 14.3 us -> 0.65 us
  other arithmetic: 10.2 us -> 0 us
    dot_general x21 -> x0, matrix products: 97.1 us -> none  [the longest x4 52.5 us: denoise(): jnp.einsum('cf,cp->fp', w_value, normed, preferred_element_type=jnp.float32)]
    pallas_call x0 -> x1, Pallas kernels: none -> 47.3 us  [shards(): pl.pallas_call(sweep, out_shape=(jax.ShapeDtypeStruct(latents.shape, f32)...]
    all_gather x1 -> x0, waiting for transfers between devices: 37.4 us -> none  [from_root(): lax.all_gather(x, axis)]
    all_gather x3 -> x0, blocking collectives: 36.8 us -> none  [entering(): pieces = lax.all_gather(total, axis)]
    ppermute x6 -> x0, waiting for transfers between devices: 29.4 us -> none  [from_behind(): return lax.ppermute(block, axis, route)]
    ppermute x6 -> x0, starting transfers between devices: 17.3 us -> none  [from_behind(): return lax.ppermute(block, axis, route)]
    all_to_all x2 -> x0, waiting for transfers between devices: 9.94 us -> none  [the longest x1 5.26 us: sent_to_all(): lax.all_to_all(jnp.broadcast_to(x[None], (peers, *x.shape)), axis, 0, 0,...]
    all_to_all x2 -> x0, starting transfers between devices: 8.78 us -> none  [the longest x1 4.81 us: summed_on_arrival(): parts = lax.all_to_all(cut_along(x, dim, peers), axis, 0, 0, tiled=True)]
  transfers between devices with their start and end apart: 9 -> 0, of which waited for: 9 -> 0; matrix products, arithmetic and copies ran while one was open for 1% -> 0% of each run, Pallas kernels for 0% -> 0%
where the time goes in v1:
time: 52 us; the launch traced here: 51.8 us
  Pallas kernels  47.3 us (91%)
  local copies, waits for them, and re-layouts  3.84 us (7%)
  between operations  0.65 us (1%)
    pallas_call x1, Pallas kernels, shards(): pl.pallas_call(sweep, out_shape=(jax.ShapeDtypeStruct(latents.shape, f32)...  47.3 us
    unnamed x5, local copies, waits for them, and re-layouts  3.84 us

profile of v1, /device:TPU:1, one launch (start us, length us, event | category | flops | bytes accessed | tf_op | source)
XLA Modules:
  0.0 51.8 jit_solution(15090309555708795321)
XLA Ops:
  0.6 1.5 %copy.11.w_out_ref = f32[320,4]{1,0:T(8,128)} copy(f32[320,4]{0,1:T(4,128)} %param.17) | data formatting | bytes 10240 | tf_op args[8]
  2.1 47.3 %sweep.1 = (f32[4,1,4,4096]{3,2,1,0:T(4,128)}, f32[4,1,4,1024]{3,2,1,0:T(4,128)}) custom-call(s32[4]{0:T(128)} %start.1, s32[4]{0:T(128)} %slide.1, f32[4,1,4,4096]{3,2,1,0:T(4,128)} %lat_ref.1, f32[4,1,4,4096]{3,2,1,0:T(4,128)} %noise_ref.1, f32[4,320]{1,0:T(4,128)} %w_in_ref.1, bf16[320,320]{1,0:T(8,128)(2,1)} %w_gate_ref.1, bf16[320,320]{1,0:T(8,128)(2,1)} %w_value_ref.1, ...), custom_call_target="tpu_custom_call" | custom-call | tf_op jit(solution)/shard_map/sweep/pallas_call | solution.py:309
  49.5 0.0 copy-start
  49.5 1.7 %copy.14 = f32[4,1,4,4096]{3,2,1,0:T(4,128)} copy(f32[4,1,4,4096]{3,2,1,0:T(4,128)} %get-tuple-element.4) | data formatting | bytes 524288
  51.2 0.0 copy-done
  51.2 0.6 %copy.15 = f32[4,1,4,1024]{3,2,1,0:T(4,128)} copy(f32[4,1,4,1024]{3,2,1,0:T(4,128)S(1)} %copy-done) | data formatting | bytes 131072
Async XLA Ops:
  49.5 1.7 %copy-start = (f32[4,1,4,1024]{3,2,1,0:T(4,128)S(1)}, f32[4,1,4,1024]{3,2,1,0:T(4,128)}, u32[]{:S(2)}) copy-start(f32[4,1,4,1024]{3,2,1,0:T(4,128)} %get-tuple-element.5) | copy-start | bytes 196612

commit v2 on v1

--- a/solution.py
+++ b/solution.py
@@ -10,7 +10,9 @@
 
 TSTEPS = 1000
 TILE = 512
+UNROLL = 8
 SLOTS = 64
+SCANNERS = 16
 HIGHEST = lax.Precision.HIGHEST
 MESH = pl.DeviceIdType.MESH
 
@@ -35,10 +37,6 @@
             x = x * pltpu.roll(x, step, axis)
             step *= 2
     return x
-
-
-def scanner_of(prompt, lat):
-    return (2 * lat + prompt % 2) * 8 + 2 * prompt + 1
 
 
 def sweep(
@@ -66,7 +64,10 @@
         pl.semaphore_signal(
             barrier, inc=1, device_id={"tm": i, "mp": lax.rem(m + k, 4)}, device_id_type=MESH
         )
-    lax.fori_loop(1, SLOTS, greet, 0)
+
+    @pl.when(i < SCANNERS)
+    def _():
+        lax.fori_loop(1, SLOTS, greet, 0)
 
     row8 = lax.broadcasted_iota(jnp.int32, (8, channels), 0)
     lane8 = lax.broadcasted_iota(jnp.int32, (8, channels), 1)
@@ -84,15 +85,14 @@
     centred = rows - jnp.mean(rows, axis=1, keepdims=True)
     gram[...] = contract_last(centred, centred) * (1.0 / channels)
 
-    w_out = jnp.concatenate(
-        [w_out_ref[...], jnp.zeros((channels, 124), jnp.float32)], axis=1
-    )
-    w_out_t = jnp.transpose(w_out)[:8, :]
+    w_out = w_out_ref[...]
+    w_out_t = jnp.where(row8 < 4, jnp.concatenate([w_out, w_out], axis=0), 0.0)
     base_row[...] = contract_last(w_out_t, rows)
 
     def three_rows(x):
         return jnp.concatenate(split3(x) + (jnp.zeros_like(x),), axis=0).astype(jnp.bfloat16)
 
+    rowk = lax.broadcasted_iota(jnp.int32, (8, hidden), 0)
     lefts = three_rows(centred)
     tables = []
     for w_ref in (w_gate_ref, w_value_ref):
@@ -104,9 +104,10 @@
     )
     folded = pieces[0:8] + pieces[8:16] + pieces[16:24]
     high, mid, low = split3(folded)
-    down[...] = jnp.concatenate([high, mid, low, jnp.zeros_like(low)], axis=0).astype(jnp.bfloat16)
-
-    rowk = lax.broadcasted_iota(jnp.int32, (8, hidden), 0)
+    down[...] = jnp.concatenate(
+        [jnp.where(rowk < 4, high, pltpu.roll(mid, 4, 0)), low], axis=0
+    ).astype(jnp.bfloat16)
+
     for p in range(prompts):
         for q, table in enumerate(tables):
             own = jnp.where(
@@ -162,12 +163,12 @@
             v = both[hidden:]
             act = (g * v * (1.0 + lax.erf(g))).astype(jnp.bfloat16)
             got = jnp.dot(inner, act, preferred_element_type=jnp.float32)
-            got = got[0:8] + got[8:16] + got[16:24]
+            got = got[0:8] + got[8:16]
             per = share // TILE
-            part[p, n // per, :, pl.ds(pl.multiple_of(lax.rem(n, per) * TILE, TILE), TILE)] = got[0:4]
+            part[p, n // per, :, pl.ds(pl.multiple_of(lax.rem(n, per) * TILE, TILE), TILE)] = got[0:4] + got[4:8]
             return carry
 
-        lax.fori_loop(0, pos // TILE, tile, 0)
+        lax.fori_loop(0, pos // TILE, tile, 0, unroll=UNROLL)
 
     def send_parts(p):
         for k in (1, 2, 3):
@@ -195,30 +196,66 @@
         for s in range(8):
             lanes = slice(s * 128, (s + 1) * 128)
             term = (cur[:, lanes] - c1 * total[:, lanes]) * c2 + c3 * nz[:, lanes] - cur[:, lanes]
-            drift[p, :, s, :] = term + head * cur[:, lanes]
-        for a in range(lats):
-            target = scanner_of(p, a)
-
-            @pl.when(i != target)
-            def _():
-                pltpu.make_async_remote_copy(
-                    src_ref=drift.at[p, a], dst_ref=slots_in.at[i],
-                    send_sem=one_send, recv_sem=one_recv,
-                    device_id={"tm": target, "mp": m}, device_id_type=MESH,
-                ).start()
-
-            @pl.when(i == target)
-            def _():
-                slots_in[SLOTS] = drift[p, a]
-
-    pl_core = lax.rem(i, 2)
-    my_prompt = lax.rem(i // 2, 4)
-    my_z = i // 8
-    my_lat = my_z // 2
-    scanning = jnp.logical_and(pl_core == 1, lax.rem(my_z, 2) == lax.rem(my_prompt, 2))
+            drift[p, :, s // 2, s % 2, :] = term + head * cur[:, lanes]
+
+        def hand_over(n):
+            pltpu.make_async_remote_copy(
+                src_ref=drift.at[p, n // 4, lax.rem(n, 4)], dst_ref=slots_in.at[p, i],
+                send_sem=one_send, recv_sem=one_recv.at[p],
+                device_id={"tm": n, "mp": m}, device_id_type=MESH,
+            ).start()
+
+        @pl.when(i >= SCANNERS)
+        def _():
+            for n in range(SCANNERS):
+                hand_over(jnp.int32(n))
+
+        @pl.when(i < SCANNERS)
+        def _():
+            def step(k, carry):
+                hand_over(lax.rem(i + k, SCANNERS))
+                return carry
+
+            lax.fori_loop(1, SCANNERS, step, 0)
+            slots_in[p, SLOTS] = drift[p, i // 4, lax.rem(i, 4)]
+
+    def scan(p):
+        settle(slots_in.at[p, pl.ds(0, SLOTS - 1)], one_recv.at[p])
+        slots_in[p, i] = slots_in[p, SLOTS]
+        acc = slots_in[p, 0]
+        sums[1] = acc
+        for j in range(1, SLOTS - 1):
+            acc = acc + slots_in[p, j]
+            sums[j + 1] = acc
+        by = slide[p]
+        for j in range(SLOTS):
+            picked[p, j] = sums[jnp.minimum(j + by, SLOTS - 1)]
+
+        def deliver(k, carry):
+            peer = lax.rem(i + k, SLOTS)
+            pltpu.make_async_remote_copy(
+                src_ref=picked.at[p, peer], dst_ref=whole.at[p, m, i // 4, lax.rem(i, 4)],
+                send_sem=two_send, recv_sem=two_recv.at[p],
+                device_id={"tm": peer, "mp": m}, device_id_type=MESH,
+            ).start()
+            return carry
+
+        lax.fori_loop(1, SLOTS, deliver, 0)
+        whole[p, m, i // 4, lax.rem(i, 4)] = picked[p, i]
+
+    def settle(ref, sem):
+        pltpu.make_async_copy(ref, ref, sem).wait()
 
     denoise(0)
-    pl.semaphore_wait(barrier, SLOTS - 1 + 3)
+
+    @pl.when(i < SCANNERS)
+    def _():
+        pl.semaphore_wait(barrier, SCANNERS - 1 + 3)
+
+    @pl.when(i >= SCANNERS)
+    def _():
+        pl.semaphore_wait(barrier, SCANNERS + 3)
+
     send_parts(0)
     for p in range(1, prompts):
         denoise(p)
@@ -226,45 +263,20 @@
         finish(p - 1)
     finish(prompts - 1)
 
-    @pl.when(scanning)
-    def _():
-        pltpu.make_async_copy(
-            slots_in.at[pl.ds(0, SLOTS - 1)], slots_in.at[pl.ds(0, SLOTS - 1)], one_recv
-        ).wait()
-        slots_in[i] = slots_in[SLOTS]
-        acc = slots_in[0]
-        sums[1] = acc
-        for j in range(1, SLOTS - 1):
-            acc = acc + slots_in[j]
-            sums[j + 1] = acc
-        by = slide[my_prompt]
-        for j in range(SLOTS):
-            picked[j] = sums[jnp.minimum(j + by, SLOTS - 1)]
-
-        def deliver(k, carry):
-            peer = lax.rem(i + k, SLOTS)
-            pltpu.make_async_remote_copy(
-                src_ref=picked.at[peer], dst_ref=whole.at[my_prompt, m, my_lat],
-                send_sem=two_send, recv_sem=two_recv.at[my_prompt],
-                device_id={"tm": peer, "mp": m}, device_id_type=MESH,
-            ).start()
-            return carry
-
-        lax.fori_loop(1, SLOTS, deliver, 0)
-        whole[my_prompt, m, my_lat] = picked[i]
-
-    for p in range(prompts):
-        mine = jnp.logical_and(scanning, my_prompt == p)
-
-        @pl.when(mine)
+    @pl.when(i < SCANNERS)
+    def _():
+        for p in range(prompts):
+            scan(p)
+
+    for p in range(prompts):
+
+        @pl.when(i < SCANNERS)
         def _():
-            pltpu.make_async_copy(
-                whole.at[p, m, pl.ds(0, lats - 1)], whole.at[p, m, pl.ds(0, lats - 1)], two_recv.at[p]
-            ).wait()
-
-        @pl.when(jnp.logical_not(mine))
+            settle(slots_in.at[p, pl.ds(0, SCANNERS - 1)], two_recv.at[p])
+
+        @pl.when(i >= SCANNERS)
         def _():
-            pltpu.make_async_copy(whole.at[p, m], whole.at[p, m], two_recv.at[p]).wait()
+            settle(slots_in.at[p, pl.ds(0, SCANNERS)], two_recv.at[p])
 
         for k in (1, 2, 3):
             peer = lax.rem(m + k, 4)
@@ -280,22 +292,19 @@
         ).wait()
         for q in range(4):
             for s in range(8):
-                out_ref[p, 0, :, q * share + s * 128 : q * share + (s + 1) * 128] = whole[p, q, :, s, :]
-
-    def settle(ref, sem):
-        pltpu.make_async_copy(ref, ref, sem).wait()
+                out_ref[p, 0, :, q * share + s * 128 : q * share + (s + 1) * 128] = whole[p, q, :, s // 2, s % 2, :]
 
     settle(part_in, part_send)
     settle(whole.at[:, pl.ds(0, 3)], all_send)
 
-    @pl.when(scanning)
-    def _():
-        settle(slots_in.at[pl.ds(0, SLOTS - 1)], two_send)
-        settle(slots_in.at[pl.ds(0, prompts * lats - 1)], one_send)
-
-    @pl.when(jnp.logical_not(scanning))
-    def _():
-        settle(slots_in.at[pl.ds(0, prompts * lats)], one_send)
+    @pl.when(i < SCANNERS)
+    def _():
+        settle(slots_in.at[:, pl.ds(0, SLOTS - 1)], two_send)
+        settle(slots_in.at[:, pl.ds(0, SCANNERS - 1)], one_send)
+
+    @pl.when(i >= SCANNERS)
+    def _():
+        settle(slots_in.at[:, pl.ds(0, SCANNERS)], one_send)
 
 
 def shards(latents, noise, start_step, slide, w_in, w_gate, w_value, w_down, w_out):
@@ -316,22 +325,22 @@
         out_specs=(vmem, vmem),
         scratch_shapes=[
             pltpu.VMEM((prompts, 2 * hidden, 128), jnp.bfloat16),
-            pltpu.VMEM((32, hidden), jnp.bfloat16),
+            pltpu.VMEM((16, hidden), jnp.bfloat16),
             pltpu.VMEM((8, 8), f32),
             pltpu.VMEM((8, 8), f32),
             pltpu.VMEM((prompts, 3, 8, 128), f32),
             pltpu.VMEM((prompts, 4, lats, share), f32),
             pltpu.VMEM((prompts, 3, lats, share), f32),
-            pltpu.VMEM((prompts, lats, 8, 128), f32),
-            pltpu.VMEM((SLOTS + 1, 8, 128), f32),
-            pltpu.VMEM((SLOTS, 8, 128), f32),
-            pltpu.VMEM((SLOTS, 8, 128), f32),
-            pltpu.VMEM((prompts, 4, lats, 8, 128), f32),
-            dma, dma((prompts,)), dma, dma, dma, dma((prompts,)), dma, dma((prompts,)),
+            pltpu.VMEM((prompts, lats, 4, 2, 128), f32),
+            pltpu.VMEM((prompts, SLOTS + 1, 2, 128), f32),
+            pltpu.VMEM((SLOTS, 2, 128), f32),
+            pltpu.VMEM((prompts, SLOTS, 2, 128), f32),
+            pltpu.VMEM((prompts, 4, lats, 4, 2, 128), f32),
+            dma, dma((prompts,)), dma, dma((prompts,)), dma, dma((prompts,)), dma, dma((prompts,)),
         ],
         compiler_params=pltpu.CompilerParams(collective_id=0, has_side_effects=True),
         name="sweep",
-    )(start_step, slide, latents, noise, w_in, w_gate, w_value, w_down, w_out)
+    )(start_step, slide, latents, noise, w_in, w_gate, w_value, w_down, w_out.T)
 
 
 def solution(mesh):

time: 52 us -> 42.9 us (0.82)
  Pallas kernels: 47.3 us -> 39.7 us
  local copies, waits for them, and re-layouts: 3.84 us -> 2.34 us
    pallas_call x1, Pallas kernels: 47.3 us -> 39.7 us  [shards(): pl.pallas_call(sweep, out_shape=(jax.ShapeDtypeStruct(latents.shape, f32)...]
    unnamed x5 -> x4, local copies, waits for them, and re-layouts: 3.84 us -> 2.34 us
where the time goes in v2:
time: 42.9 us; the launch traced here: 42.7 us
  Pallas kernels  39.7 us (93%)
  local copies, waits for them, and re-layouts  2.34 us (5%)
  between operations  0.65 us (2%)
    pallas_call x1, Pallas kernels, shards(): pl.pallas_call(sweep, out_shape=(jax.ShapeDtypeStruct(latents.shape, f32)...  39.7 us
    unnamed x4, local copies, waits for them, and re-layouts  2.34 us

profile of v2, /device:TPU:1, one launch (start us, length us, event | category | flops | bytes accessed | tf_op | source)
XLA Modules:
  0.0 42.7 jit_solution(15325542644779843063)
XLA Ops:
  0.6 39.7 %sweep.1 = (f32[4,1,4,4096]{3,2,1,0:T(4,128)}, f32[4,1,4,1024]{3,2,1,0:T(4,128)}) custom-call(s32[4]{0:T(128)} %start.1, s32[4]{0:T(128)} %slide.1, f32[4,1,4,4096]{3,2,1,0:T(4,128)} %lat_ref.1, f32[4,1,4,4096]{3,2,1,0:T(4,128)} %noise_ref.1, f32[4,320]{1,0:T(4,128)} %w_in_ref.1, bf16[320,320]{1,0:T(8,128)(2,1)} %w_gate_ref.1, bf16[320,320]{1,0:T(8,128)(2,1)} %w_value_ref.1, ...), custom_call_target="tpu_custom_call" | custom-call | tf_op jit(solution)/shard_map/sweep/pallas_call | solution.py:318
  40.4 0.0 copy-start
  40.4 1.7 %copy.13 = f32[4,1,4,4096]{3,2,1,0:T(4,128)} copy(f32[4,1,4,4096]{3,2,1,0:T(4,128)} %get-tuple-element.4) | data formatting | bytes 524288
  42.1 0.0 copy-done
  42.1 0.6 %copy.14 = f32[4,1,4,1024]{3,2,1,0:T(4,128)} copy(f32[4,1,4,1024]{3,2,1,0:T(4,128)S(1)} %copy-done) | data formatting | bytes 131072
Async XLA Ops:
  40.4 1.7 %copy-start = (f32[4,1,4,1024]{3,2,1,0:T(4,128)S(1)}, f32[4,1,4,1024]{3,2,1,0:T(4,128)}, u32[]{:S(2)}) copy-start(f32[4,1,4,1024]{3,2,1,0:T(4,128)} %get-tuple-element.5) | copy-start | bytes 196612

commit v3 on v2

--- a/solution.py
+++ b/solution.py
@@ -9,8 +9,8 @@
 from jax.sharding import PartitionSpec as P
 
 TSTEPS = 1000
-TILE = 512
-UNROLL = 8
+TILE = 2048
+UNROLL = 2
 SLOTS = 64
 SCANNERS = 16
 HIGHEST = lax.Precision.HIGHEST
@@ -117,7 +117,8 @@
             stack = jnp.concatenate(
                 [high, high, mid, mid, high, low, jnp.zeros((80, hidden), jnp.float32)], axis=0
             )
-            lhs[p, q * hidden : (q + 1) * hidden, :] = jnp.transpose(stack).astype(jnp.bfloat16)
+            turned = jnp.transpose(stack).astype(jnp.bfloat16)
+            lhs[p, :, q] = turned.reshape(hidden // 16, 16, 128)
 
     grid = (
         lax.broadcasted_iota(jnp.int32, (8, 128), 0) * 128
@@ -140,7 +141,7 @@
 
     def denoise(p):
         cov = gram[...]
-        left = lhs[p]
+        left = lhs[p].reshape(2 * hidden, 128)
         inner = down[...]
 
         def tile(n, carry):
@@ -159,13 +160,16 @@
                 [high, mid, high, mid, low, high, jnp.zeros((80, TILE), jnp.float32)], axis=0
             ).astype(jnp.bfloat16)
             both = jnp.dot(left, right, preferred_element_type=jnp.float32)
-            g = both[:hidden]
-            v = both[hidden:]
-            act = (g * v * (1.0 + lax.erf(g))).astype(jnp.bfloat16)
+            both = both.reshape(hidden // 16, 2, 16, TILE)
+            g = both[:, 0]
+            v = both[:, 1]
+            act = (g * v * (1.0 + lax.erf(g))).astype(jnp.bfloat16).reshape(hidden, TILE)
             got = jnp.dot(inner, act, preferred_element_type=jnp.float32)
             got = got[0:8] + got[8:16]
-            per = share // TILE
-            part[p, n // per, :, pl.ds(pl.multiple_of(lax.rem(n, per) * TILE, TILE), TILE)] = got[0:4] + got[4:8]
+            per = TILE // share
+            for u in range(per):
+                w = got[:, u * share : (u + 1) * share]
+                part[p, n * per + u] = w[0:4] + w[4:8]
             return carry
 
         lax.fori_loop(0, pos // TILE, tile, 0, unroll=UNROLL)
@@ -318,13 +322,13 @@
     return pl.pallas_call(
         sweep,
         out_shape=(
-            jax.ShapeDtypeStruct(latents.shape, f32),
-            jax.ShapeDtypeStruct((prompts, 1, lats, share), f32),
+            pltpu.VMEM(latents.shape, f32),
+            pltpu.VMEM((prompts, 1, lats, share), f32),
         ),
         in_specs=[smem, smem] + [vmem] * 7,
         out_specs=(vmem, vmem),
         scratch_shapes=[
-            pltpu.VMEM((prompts, 2 * hidden, 128), jnp.bfloat16),
+            pltpu.VMEM((prompts, hidden // 16, 2, 16, 128), jnp.bfloat16),
             pltpu.VMEM((16, hidden), jnp.bfloat16),
             pltpu.VMEM((8, 8), f32),
             pltpu.VMEM((8, 8), f32),

time: 42.9 us -> 38.8 us (0.904)
  Pallas kernels: 39.7 us -> 36.7 us
  local copies, waits for them, and re-layouts: 2.34 us -> 1.33 us
    pallas_call x1, Pallas kernels: 39.7 us -> 36.7 us  [shards(): pl.pallas_call(sweep, out_shape=(pltpu.VMEM(latents.shape, f32), pltpu.VM...]
    unnamed x4 -> x2, local copies, waits for them, and re-layouts: 2.34 us -> 1.33 us
where the time goes in v3:
time: 38.8 us; the launch traced here: 38.7 us
  Pallas kernels  36.7 us (95%)
  local copies, waits for them, and re-layouts  1.33 us (3%)
  between operations  0.64 us (2%)
    pallas_call x1, Pallas kernels, shards(): pl.pallas_call(sweep, out_shape=(pltpu.VMEM(latents.shape, f32), pltpu.VM...  36.7 us
    unnamed x2, local copies, waits for them, and re-layouts  1.33 us

profile of v3, /device:TPU:1, one launch (start us, length us, event | category | flops | bytes accessed | tf_op | source)
XLA Modules:
  0.0 38.7 jit_solution(6855879784504968367)
XLA Ops:
  0.6 36.7 %sweep.1 = (f32[4,1,4,4096]{3,2,1,0:T(4,128)S(1)}, f32[4,1,4,1024]{3,2,1,0:T(4,128)S(1)}) custom-call(s32[4]{0:T(128)} %start.1, s32[4]{0:T(128)} %slide.1, f32[4,1,4,4096]{3,2,1,0:T(4,128)} %lat_ref.1, f32[4,1,4,4096]{3,2,1,0:T(4,128)} %noise_ref.1, f32[4,320]{1,0:T(4,128)} %w_in_ref.1, bf16[320,320]{1,0:T(8,128)(2,1)} %w_gate_ref.1, ...), custom_call_target="tpu_custom_call" | custom-call | tf_op jit(solution)/shard_map/sweep/pallas_call | solution.py:322
  37.4 0.7 %copy.13 = f32[4,1,4,4096]{3,2,1,0:T(4,128)} copy(f32[4,1,4,4096]{3,2,1,0:T(4,128)S(1)} %get-tuple-element.2) | data formatting | bytes 524288
  38.1 0.6 %copy.14 = f32[4,1,4,1024]{3,2,1,0:T(4,128)} copy(f32[4,1,4,1024]{3,2,1,0:T(4,128)S(1)} %get-tuple-element.3) | data formatting | bytes 131072

commit v4 on v3

v4 whole, which is shorter than its diff:
```python
import functools
import math

import jax
import jax.numpy as jnp
from jax import lax
from jax.experimental import pallas as pl
from jax.experimental.pallas import tpu as pltpu
from jax.sharding import PartitionSpec as P

TSTEPS = 1000
TILE = 2048
SLOTS = 64
SCANNERS = 8
NEAR = 16
EARLY = 2
HIGHEST = lax.Precision.HIGHEST
MESH = pl.DeviceIdType.MESH


def split3(x):
    high = x.astype(jnp.bfloat16).astype(jnp.float32)
    rest = x - high
    mid = rest.astype(jnp.bfloat16).astype(jnp.float32)
    return high, mid, rest - mid


def contract_last(a, b):
    return lax.dot_general(
        a, b, (((1,), (1,)), ((), ())), precision=HIGHEST, preferred_element_type=jnp.float32
    )


def product_all(x):
    for axis, extent in ((1, 128), (0, 8)):
        step = 1
        while step < extent:
            x = x * pltpu.roll(x, step, axis)
            step *= 2
    return x


def sweep(
    start, slide, lat_ref, noise_ref, w_in_ref, w_gate_ref, w_value_ref, w_down_ref, w_out_ref,
    out_ref, eps_ref,
    lhs, down, rights, scaled, begun, table, table_in, base_row, gram, coef, part, part_in, drift, slots_in, sums, picked, whole,
    table_send, table_recv, part_send, part_recv, one_send, one_recv, two_send, two_recv, all_send, all_recv,
):
    prompts, _, lats, pos = lat_ref.shape
    channels = w_in_ref.shape[1]
    hidden = w_gate_ref.shape[1]
    share = pos // 4
    i = lax.axis_index("tm")
    m = lax.axis_index("mp")
    turn = i // 2
    scanning = jnp.logical_and(lax.rem(i, 2) == 1, i < 2 * SCANNERS)
    resting = jnp.logical_not(scanning)
    own_lat = turn // 2
    own_half = lax.rem(turn, 2)

    barrier = pltpu.get_barrier_semaphore()

    def greet(k, carry):
        pl.semaphore_signal(
            barrier, inc=1, device_id={"tm": lax.rem(i + k, SLOTS), "mp": m}, device_id_type=MESH
        )
        return carry

    for k in (1, 2, 3):
        pl.semaphore_signal(
            barrier, inc=1, device_id={"tm": i, "mp": lax.rem(m + k, 4)}, device_id_type=MESH
        )

    @pl.when(scanning)
    def _():
        lax.fori_loop(1, SLOTS, greet, 0)

    row8 = lax.broadcasted_iota(jnp.int32, (8, channels), 0)
    lane8 = lax.broadcasted_iota(jnp.int32, (8, channels), 1)
    half = channels // 2
    steps = jnp.zeros((8, channels), jnp.int32)
    for p in range(prompts):
        steps = jnp.where(row8 == 4 + p, start[p] - i, steps)
    freq = jnp.exp(
        -math.log(10000.0) * jnp.where(lane8 < half, lane8, lane8 - half).astype(jnp.float32) / half
    )
    angle = steps.astype(jnp.float32) * freq
    emb = jnp.where(lane8 < half, jnp.cos(angle), jnp.sin(angle))
    w_in = w_in_ref[...]
    rows = jnp.where(row8 < 4, jnp.concatenate([w_in, w_in], axis=0), emb)
    centred = rows - jnp.mean(rows, axis=1, keepdims=True)
    gram[...] = contract_last(centred, centred) * (1.0 / channels)

    w_out = w_out_ref[...]
    w_out_t = jnp.where(row8 < 4, jnp.concatenate([w_out, w_out], axis=0), 0.0)
    base_row[...] = contract_last(w_out_t, rows)

    def three_rows(x):
        return jnp.concatenate(split3(x) + (jnp.zeros_like(x),), axis=0).astype(jnp.bfloat16)

    rowk = lax.broadcasted_iota(jnp.int32, (8, hidden), 0)
    lefts = three_rows(centred)
    tables = []
    for w_ref in (w_gate_ref, w_value_ref):
        pieces = jnp.dot(lefts, w_ref[...], preferred_element_type=jnp.float32)
        tables.append((pieces[0:8] + pieces[8:16] + pieces[16:24]) * math.sqrt(0.5))
    pieces = lax.dot_general(
        three_rows(w_out_t), w_down_ref[...], (((1,), (1,)), ((), ())),
        preferred_element_type=jnp.float32,
    )
    folded = pieces[0:8] + pieces[8:16] + pieces[16:24]
    table[0:8] = jnp.where(rowk < 4, tables[0], pltpu.roll(tables[1], 4, 0))
    gates = pltpu.roll(tables[0], 8 - 4 - EARLY, 0)
    values = pltpu.roll(tables[1], 8 - 4 - EARLY + 2, 0)
    table[8:16] = jnp.where(
        rowk < 2, gates, jnp.where(rowk < 4, values, pltpu.roll(folded, 4, 0))
    )

    @pl.when(scanning)
    def _():
        pl.semaphore_wait(barrier, SCANNERS - 1 + 3)

    @pl.when(resting)
    def _():
        pl.semaphore_wait(barrier, SCANNERS + 3)

    for k in (1, 2, 3):
        pltpu.make_async_remote_copy(
            src_ref=table, dst_ref=table_in.at[k - 1],
            send_sem=table_send, recv_sem=table_recv,
            device_id={"tm": i, "mp": lax.rem(m + k, 4)}, device_id_type=MESH,
        ).start()

    def set_left(place, p, gate, value, folded):
        own = jnp.where(rowk < 4, gate, jnp.where(rowk == 4, gate[4 + p : 5 + p, :], 0.0))
        high, mid, low = split3(own)
        stack = jnp.concatenate(
            [high, high, mid, mid, high, low, jnp.zeros((80, hidden), jnp.float32)], axis=0
        )
        turned = jnp.transpose(stack).astype(jnp.bfloat16)
        lhs[place] = turned.reshape(hidden // 16, 16, 128)
        twice = jnp.where(rowk < 4, folded, pltpu.roll(folded, 4, 0))
        levels = [split3(twice * value[r : r + 1, :]) for r in (0, 1, 2, 3, 4 + p)]
        blocks = [levels[r][level] for level in range(3) for r in range(5)]
        blocks.append(jnp.zeros_like(twice))
        down[place] = jnp.concatenate(
            [jnp.where(rowk < 4, blocks[2 * j], blocks[2 * j + 1]) for j in range(8)], axis=0
        ).astype(jnp.bfloat16)

    def place_of(p, k):
        return p if p < EARLY else EARLY + 4 * (p - EARLY) + k

    for p in range(prompts):
        set_left(place_of(p, 0), p, tables[0], tables[1], folded)

    grid = (
        lax.broadcasted_iota(jnp.int32, (8, 128), 0) * 128
        + lax.broadcasted_iota(jnp.int32, (8, 128), 1)
    )

    def beta_at(k):
        return 0.0001 + (0.02 - 0.0001) * k.astype(jnp.float32) / (TSTEPS - 1)

    kept = 1.0 - beta_at(grid)
    for p in range(prompts):
        t = jnp.full((8, 128), start[p] - i, jnp.int32)
        abar = product_all(jnp.where(grid <= t, kept, 1.0))
        beta = beta_at(t)
        coef[p, 0] = beta / jnp.sqrt(1.0 - abar)
        coef[p, 1] = 1.0 / jnp.sqrt(1.0 - beta)
        coef[p, 2] = jnp.sqrt(beta)

    def rescaled(p, x4):
        cov = gram[...]
        width = x4.shape[1]
        rowt = lax.broadcasted_iota(jnp.int32, (8, width), 0)
        x8 = jnp.concatenate([x4, x4], axis=0)
        x = jnp.where(rowt < 4, x8, 0.0)
        z = jnp.zeros((8, width), jnp.float32) + 2.0 * cov[:, 4 + p : 5 + p]
        for b in range(4):
            z = z + cov[:, b : b + 1] * x4[b : b + 1, :]
        var = jnp.sum(x * z, axis=0, keepdims=True) + cov[4 + p : 5 + p, 4 + p : 5 + p]
        scale = lax.rsqrt(var + 1e-05)
        y = jnp.where(rowt < 4, x8, jnp.where(rowt == 4, 1.0, 0.0)) * scale
        high, mid, low = split3(y)
        right = jnp.concatenate(
            [high, mid, high, mid, low, high, jnp.zeros((80, width), jnp.float32)], axis=0
        ).astype(jnp.bfloat16)
        return y, right

    def through(place, right):
        left = lhs[place].reshape(hidden, 128)
        g = jnp.dot(left, right, preferred_element_type=jnp.float32)
        act = (g * (1.0 + lax.erf(g))).astype(jnp.bfloat16)
        return jnp.dot(down[place], act, preferred_element_type=jnp.float32)

    def weighed(got, y):
        rowt = lax.broadcasted_iota(jnp.int32, y.shape, 0)
        total = jnp.zeros_like(y)
        for j in range(8):
            a, b = 2 * j % 5, (2 * j + 1) % 5
            total = total + got[8 * j : 8 * j + 8] * jnp.where(rowt < 4, y[a : a + 1], y[b : b + 1])
        return total[0:4] + total[4:8]

    def denoise(p, n):
        y, right = rescaled(p, lat_ref[p, 0, :, n * TILE : (n + 1) * TILE])
        got = weighed(through(p, right), y)
        per = TILE // share
        for u in range(per):
            part[p, n * per + u] = got[:, u * share : (u + 1) * share]

    def denoise_first(p):
        mine = pl.ds(pl.multiple_of(m * share, share), share)
        y, right = rescaled(p, lat_ref[p, 0, :, mine])
        rights[p - EARLY] = right
        scaled[p - EARLY] = y
        begun[p - EARLY] = through(place_of(p, 0), right)

    def denoise_rest(p):
        total = begun[p - EARLY]
        for k in (1, 2, 3):
            total = total + through(place_of(p, k), rights[p - EARLY])
        return weighed(total, scaled[p - EARLY])

    def take_tables():
        settle(table_in, table_recv)
        for k in (1, 2, 3):
            common, rest = table_in[k - 1, 0:8], table_in[k - 1, 8:16]
            folded = pltpu.roll(rest, 4, 0)
            turned = pltpu.roll(common, 4, 0)
            for p in range(EARLY, prompts):
                n = p - EARLY
                gate = jnp.where(rowk < 4, common, rest[n : n + 1])
                value = jnp.where(rowk < 4, turned, rest[2 + n : 3 + n])
                set_left(place_of(p, k), p, gate, value, folded)

    def send_parts(p):
        for k in (1, 2, 3):
            peer = lax.rem(m + k, 4)
            pltpu.make_async_remote_copy(
                src_ref=part.at[p, peer], dst_ref=part_in.at[p, k - 1],
                send_sem=part_send, recv_sem=part_recv.at[p],
                device_id={"tm": i, "mp": peer}, device_id_type=MESH,
            ).start()

    def summed(p):
        settle(part_in.at[p], part_recv.at[p])
        return part[p, m] + part_in[p, 0] + part_in[p, 1] + part_in[p, 2]

    def finish(p, total):
        mine = pl.ds(pl.multiple_of(m * share, share), share)
        cur = lat_ref[p, 0, :, mine]
        nz = noise_ref[p, 0, :, mine]
        for a in range(4):
            total = total + base_row[0:4, a : a + 1] * cur[a : a + 1, :]
        total = total + base_row[0:4, 4 + p : 5 + p]
        eps_ref[p, 0] = total
        c1 = coef[p, 0][0:4]
        c2 = coef[p, 1][0:4]
        c3 = coef[p, 2][0:4]
        head = jnp.where(jnp.full((4, 128), i, jnp.int32) == 0, 1.0, 0.0)
        for s in range(8):
            lanes = slice(s * 128, (s + 1) * 128)
            term = (cur[:, lanes] - c1 * total[:, lanes]) * c2 + c3 * nz[:, lanes] - cur[:, lanes]
            drift[p, :, s // 4, s % 4, :] = term + head * cur[:, lanes]

        def hand_over(n):
            pltpu.make_async_remote_copy(
                src_ref=drift.at[p, n // 2, lax.rem(n, 2)], dst_ref=slots_in.at[p, i],
                send_sem=one_send, recv_sem=one_recv.at[p],
                device_id={"tm": 2 * n + 1, "mp": m}, device_id_type=MESH,
            ).start()

        @pl.when(resting)
        def _():
            for n in range(SCANNERS):
                hand_over(jnp.int32(n))

        @pl.when(scanning)
        def _():
            def step(k, carry):
                hand_over(lax.rem(turn + k, SCANNERS))
                return carry

            lax.fori_loop(1, SCANNERS, step, 0)
            slots_in[p, SLOTS] = drift[p, own_lat, own_half]

    def deliver(p, low, high):
        def step(peer, carry):
            pltpu.make_async_remote_copy(
                src_ref=picked.at[p, peer], dst_ref=whole.at[p, m, own_lat, own_half],
                send_sem=two_send, recv_sem=two_recv.at[p],
                device_id={"tm": peer, "mp": m}, device_id_type=MESH,
            ).start()
            return carry

        lax.fori_loop(low, high, step, 0)

    def scan(p):
        settle(slots_in.at[p, pl.ds(0, SLOTS - 1)], one_recv.at[p])
        slots_in[p, i] = slots_in[p, SLOTS]
        acc = slots_in[p, 0]
        sums[1] = acc
        for j in range(1, SLOTS - 1):
            acc = acc + slots_in[p, j]
            sums[j + 1] = acc
        by = slide[p]
        for j in range(SLOTS):
            picked[p, j] = sums[jnp.minimum(j + by, SLOTS - 1)]

        deliver(p, 0, i)
        deliver(p, i + 1, NEAR)
        whole[p, m, own_lat, own_half] = picked[p, i]

    def settle(ref, sem):
        pltpu.make_async_copy(ref, ref, sem).wait()

    for p in range(EARLY):
        for n in range(pos // TILE):
            denoise(p, n)
        send_parts(p)
    for p in range(EARLY, prompts):
        denoise_first(p)
    take_tables()
    finish(2, denoise_rest(2))
    finish(0, summed(0))
    finish(1, summed(1))
    finish(3, denoise_rest(3))

    @pl.when(scanning)
    def _():
        scan(2)
        deliver(2, NEAR, SLOTS)
        scan(0)
        deliver(0, NEAR, SLOTS)
        scan(1)
        scan(3)
        deliver(1, NEAR, SLOTS)
        deliver(3, NEAR, SLOTS)

    for p in (2, 0, 1, 3):

        @pl.when(scanning)
        def _():
            settle(slots_in.at[p, pl.ds(0, SCANNERS - 1)], two_recv.at[p])

        @pl.when(resting)
        def _():
            settle(slots_in.at[p, pl.ds(0, SCANNERS)], two_recv.at[p])

        for k in (1, 2, 3):
            peer = lax.rem(m + k, 4)
            pltpu.make_async_remote_copy(
                src_ref=whole.at[p, m], dst_ref=whole.at[p, m],
                send_sem=all_send, recv_sem=all_recv.at[p],
                device_id={"tm": i, "mp": peer}, device_id_type=MESH,
            ).start()

    for p in range(prompts):
        pltpu.make_async_copy(
            whole.at[p, pl.ds(0, 3)], whole.at[p, pl.ds(0, 3)], all_recv.at[p]
        ).wait()
        for q in range(4):
            for s in range(8):
                out_ref[p, 0, :, q * share + s * 128 : q * share + (s + 1) * 128] = whole[p, q, :, s // 4, s % 4, :]

    settle(part_in, part_send)
    settle(table_in, table_send)
    settle(whole.at[:, pl.ds(0, 3)], all_send)

    @pl.when(scanning)
    def _():
        settle(slots_in.at[:, pl.ds(0, SLOTS - 1)], two_send)
        settle(slots_in.at[:, pl.ds(0, SCANNERS - 1)], one_send)

    @pl.when(resting)
    def _():
        settle(slots_in.at[:, pl.ds(0, SCANNERS)], one_send)


def shards(latents, noise, start_step, slide, w_in, w_gate, w_value, w_down, w_out):
    prompts, _, lats, pos = latents.shape
    hidden = w_gate.shape[1]
    share = pos // 4
    f32 = jnp.float32
    smem = pl.BlockSpec(memory_space=pltpu.SMEM)
    vmem = pl.BlockSpec(memory_space=pltpu.VMEM)
    dma = pltpu.SemaphoreType.DMA
    return pl.pallas_call(
        sweep,
        out_shape=(
            pltpu.VMEM(latents.shape, f32),
            pltpu.VMEM((prompts, 1, lats, share), f32),
        ),
        in_specs=[smem, smem] + [vmem] * 7,
        out_specs=(vmem, vmem),
        scratch_shapes=[
            pltpu.VMEM((EARLY + 4 * (prompts - EARLY), hidden // 16, 16, 128), jnp.bfloat16),
            pltpu.VMEM((EARLY + 4 * (prompts - EARLY), 64, hidden), jnp.bfloat16),
            pltpu.VMEM((prompts - EARLY, 128, share), jnp.bfloat16),
            pltpu.VMEM((prompts - EARLY, 8, share), f32),
            pltpu.VMEM((prompts - EARLY, 64, share), f32),
            pltpu.VMEM((16, hidden), f32),
            pltpu.VMEM((3, 16, hidden), f32),
            pltpu.VMEM((8, 8), f32),
            pltpu.VMEM((8, 8), f32),
            pltpu.VMEM((prompts, 3, 8, 128), f32),
            pltpu.VMEM((EARLY, 4, lats, share), f32),
            pltpu.VMEM((EARLY, 3, lats, share), f32),
            pltpu.VMEM((prompts, lats, 2, 4, 128), f32),
            pltpu.VMEM((prompts, SLOTS + 1, 4, 128), f32),
            pltpu.VMEM((SLOTS, 4, 128), f32),
            pltpu.VMEM((prompts, SLOTS, 4, 128), f32),
            pltpu.VMEM((prompts, 4, lats, 2, 4, 128), f32),
            dma, dma, dma, dma((EARLY,)), dma, dma((prompts,)), dma, dma((prompts,)), dma, dma((prompts,)),
        ],
        compiler_params=pltpu.CompilerParams(collective_id=0, has_side_effects=True),
        name="sweep",
    )(start_step, slide, latents, noise, w_in, w_gate, w_value, w_down, w_out.T)


def solution(mesh):
    in_specs = (
        P(None, "tm", None, None),
        P(None, "tm", None, None),
        P(),
        P(),
        P(),
        P(None, "mp"),
        P(None, "mp"),
        P("mp", None),
        P(),
    )
    out_specs = (P(None, "tm", None, None), P(None, "tm", None, "mp"))
    return jax.shard_map(shards, mesh=mesh, in_specs=in_specs, out_specs=out_specs, check_vma=False)
```

time: 38.8 us -> 33.3 us (0.86)
  Pallas kernels: 36.7 us -> 31.2 us
    pallas_call x1, Pallas kernels: 36.7 us -> 31.2 us  [shards(): pl.pallas_call(sweep, out_shape=(pltpu.VMEM(latents.shape, f32), pltpu.VM...]
where the time goes in v4:
time: 33.3 us; the launch traced here: 33.2 us
  Pallas kernels  31.2 us (94%)
  local copies, waits for them, and re-layouts  1.33 us (4%)
  between operations  0.64 us (2%)
    pallas_call x1, Pallas kernels, shards(): pl.pallas_call(sweep, out_shape=(pltpu.VMEM(latents.shape, f32), pltpu.VM...  31.2 us
    unnamed x2, local copies, waits for them, and re-layouts  1.33 us

profile of v4, /device:TPU:1, one launch (start us, length us, event | category | flops | bytes accessed | tf_op | source)
XLA Modules:
  0.0 33.2 jit_solution(3538697804925603580)
XLA Ops:
  0.6 31.2 %sweep.1 = (f32[4,1,4,4096]{3,2,1,0:T(4,128)S(1)}, f32[4,1,4,1024]{3,2,1,0:T(4,128)S(1)}) custom-call(s32[4]{0:T(128)} %start.1, s32[4]{0:T(128)} %slide.1, f32[4,1,4,4096]{3,2,1,0:T(4,128)} %lat_ref.1, f32[4,1,4,4096]{3,2,1,0:T(4,128)} %noise_ref.1, f32[4,320]{1,0:T(4,128)} %w_in_ref.1, bf16[320,320]{1,0:T(8,128)(2,1)} %w_gate_ref.1, ...), custom_call_target="tpu_custom_call" | custom-call | tf_op jit(solution)/shard_map/sweep/pallas_call | solution.py:389
  31.8 0.7 %copy.13 = f32[4,1,4,4096]{3,2,1,0:T(4,128)} copy(f32[4,1,4,4096]{3,2,1,0:T(4,128)S(1)} %get-tuple-element.2) | data formatting | bytes 524288
  32.5 0.6 %copy.14 = f32[4,1,4,1024]{3,2,1,0:T(4,128)} copy(f32[4,1,4,1024]{3,2,1,0:T(4,128)S(1)} %get-tuple-element.3) | data formatting | bytes 131072

commit v5 on v4

--- a/solution.py
+++ b/solution.py
@@ -378,6 +378,17 @@
         settle(slots_in.at[:, pl.ds(0, SCANNERS)], one_send)
 
 
+def put_out(window, eps, window_out, eps_out, sems):
+    copies = [
+        pltpu.make_async_copy(window, window_out, sems.at[0]),
+        pltpu.make_async_copy(eps, eps_out, sems.at[1]),
+    ]
+    for copy in copies:
+        copy.start()
+    for copy in copies:
+        copy.wait()
+
+
 def shards(latents, noise, start_step, slide, w_in, w_gate, w_value, w_down, w_out):
     prompts, _, lats, pos = latents.shape
     hidden = w_gate.shape[1]
@@ -385,8 +396,9 @@
     f32 = jnp.float32
     smem = pl.BlockSpec(memory_space=pltpu.SMEM)
     vmem = pl.BlockSpec(memory_space=pltpu.VMEM)
+    any_space = pl.BlockSpec(memory_space=pl.ANY)
     dma = pltpu.SemaphoreType.DMA
-    return pl.pallas_call(
+    window, eps = pl.pallas_call(
         sweep,
         out_shape=(
             pltpu.VMEM(latents.shape, f32),
@@ -417,6 +429,18 @@
         compiler_params=pltpu.CompilerParams(collective_id=0, has_side_effects=True),
         name="sweep",
     )(start_step, slide, latents, noise, w_in, w_gate, w_value, w_down, w_out.T)
+    return pl.pallas_call(
+        put_out,
+        out_shape=(
+            jax.ShapeDtypeStruct(latents.shape, f32),
+            jax.ShapeDtypeStruct((prompts, 1, lats, share), f32),
+        ),
+        in_specs=[any_space, any_space],
+        out_specs=(any_space, any_space),
+        scratch_shapes=[dma((2,))],
+        compiler_params=pltpu.CompilerParams(vmem_limit_bytes=1024 * 1024),
+        name="put_out",
+    )(window, eps)
 
 
 def solution(mesh):

time: 33.3 us -> 32.8 us (0.985)
  local copies, waits for them, and re-layouts: 1.33 us -> 0 us
  Pallas kernels: 31.2 us -> 32 us
    unnamed x2 -> x0, local copies, waits for them, and re-layouts: 1.33 us -> none
    pallas_call x0 -> x1, Pallas kernels: none -> 0.74 us  [shards(): pl.pallas_call(put_out, out_shape=(jax.ShapeDtypeStruct(latents.shape, f3...]
where the time goes in v5:
time: 32.8 us; the launch traced here: 32.7 us
  Pallas kernels  32 us (98%)
  between operations  0.64 us (2%)
    pallas_call x1, Pallas kernels, shards(): pl.pallas_call(sweep, out_shape=(pltpu.VMEM(latents.shape, f32), pltpu.VM...  31.3 us
    pallas_call x1, Pallas kernels, shards(): pl.pallas_call(put_out, out_shape=(jax.ShapeDtypeStruct(latents.shape, f3...  0.74 us

profile of v5, /device:TPU:1, one launch (start us, length us, event | category | flops | bytes accessed | tf_op | source)
XLA Modules:
  0.0 32.7 jit_solution(15080629603578328378)
XLA Ops:
  0.6 31.3 %sweep.1 = (f32[4,1,4,4096]{3,2,1,0:T(4,128)S(1)}, f32[4,1,4,1024]{3,2,1,0:T(4,128)S(1)}) custom-call(s32[4]{0:T(128)} %start.1, s32[4]{0:T(128)} %slide.1, f32[4,1,4,4096]{3,2,1,0:T(4,128)} %lat_ref.1, f32[4,1,4,4096]{3,2,1,0:T(4,128)} %noise_ref.1, f32[4,320]{1,0:T(4,128)} %w_in_ref.1, bf16[320,320]{1,0:T(8,128)(2,1)} %w_gate_ref.1, ...), custom_call_target="tpu_custom_call" | custom-call | tf_op jit(solution)/shard_map/sweep/pallas_call | solution.py:401
  31.9 0.7 %put_out.1 = (f32[4,1,4,4096]{3,2,1,0:T(4,128)}, f32[4,1,4,1024]{3,2,1,0:T(4,128)}) custom-call(f32[4,1,4,4096]{3,2,1,0:T(4,128)S(1)} %get-tuple-element.4.window, f32[4,1,4,1024]{3,2,1,0:T(4,128)S(1)} %get-tuple-element.5.eps), custom_call_target="tpu_custom_call" | custom-call | tf_op jit(solution)/shard_map/put_out/pallas_call | solution.py:432

commit v6 on v5

--- a/solution.py
+++ b/solution.py
@@ -12,8 +12,6 @@
 TILE = 2048
 SLOTS = 64
 SCANNERS = 8
-NEAR = 16
-EARLY = 2
 HIGHEST = lax.Precision.HIGHEST
 MESH = pl.DeviceIdType.MESH
 
@@ -43,8 +41,8 @@
 def sweep(
     start, slide, lat_ref, noise_ref, w_in_ref, w_gate_ref, w_value_ref, w_down_ref, w_out_ref,
     out_ref, eps_ref,
-    lhs, down, rights, scaled, begun, table, table_in, base_row, gram, coef, part, part_in, drift, slots_in, sums, picked, whole,
-    table_send, table_recv, part_send, part_recv, one_send, one_recv, two_send, two_recv, all_send, all_recv,
+    lhs, down, base_row, gram, coef, part, part_in, drift, slots_in, sums, picked, whole,
+    part_send, part_recv, one_send, one_recv, two_send, two_recv, all_send, all_recv,
 ):
     prompts, _, lats, pos = lat_ref.shape
     channels = w_in_ref.shape[1]
@@ -109,28 +107,6 @@
         preferred_element_type=jnp.float32,
     )
     folded = pieces[0:8] + pieces[8:16] + pieces[16:24]
-    table[0:8] = jnp.where(rowk < 4, tables[0], pltpu.roll(tables[1], 4, 0))
-    gates = pltpu.roll(tables[0], 8 - 4 - EARLY, 0)
-    values = pltpu.roll(tables[1], 8 - 4 - EARLY + 2, 0)
-    table[8:16] = jnp.where(
-        rowk < 2, gates, jnp.where(rowk < 4, values, pltpu.roll(folded, 4, 0))
-    )
-
-    @pl.when(scanning)
-    def _():
-        pl.semaphore_wait(barrier, SCANNERS - 1 + 3)
-
-    @pl.when(resting)
-    def _():
-        pl.semaphore_wait(barrier, SCANNERS + 3)
-
-    for k in (1, 2, 3):
-        pltpu.make_async_remote_copy(
-            src_ref=table, dst_ref=table_in.at[k - 1],
-            send_sem=table_send, recv_sem=table_recv,
-            device_id={"tm": i, "mp": lax.rem(m + k, 4)}, device_id_type=MESH,
-        ).start()
-
     def set_left(place, p, gate, value, folded):
         own = jnp.where(rowk < 4, gate, jnp.where(rowk == 4, gate[4 + p : 5 + p, :], 0.0))
         high, mid, low = split3(own)
@@ -147,11 +123,8 @@
             [jnp.where(rowk < 4, blocks[2 * j], blocks[2 * j + 1]) for j in range(8)], axis=0
         ).astype(jnp.bfloat16)
 
-    def place_of(p, k):
-        return p if p < EARLY else EARLY + 4 * (p - EARLY) + k
-
-    for p in range(prompts):
-        set_left(place_of(p, 0), p, tables[0], tables[1], folded)
+    for p in range(prompts):
+        set_left(p, p, tables[0], tables[1], folded)
 
     grid = (
         lax.broadcasted_iota(jnp.int32, (8, 128), 0) * 128
@@ -209,33 +182,8 @@
         for u in range(per):
             part[p, n * per + u] = got[:, u * share : (u + 1) * share]
 
-    def denoise_first(p):
-        mine = pl.ds(pl.multiple_of(m * share, share), share)
-        y, right = rescaled(p, lat_ref[p, 0, :, mine])
-        rights[p - EARLY] = right
-        scaled[p - EARLY] = y
-        begun[p - EARLY] = through(place_of(p, 0), right)
-
-    def denoise_rest(p):
-        total = begun[p - EARLY]
-        for k in (1, 2, 3):
-            total = total + through(place_of(p, k), rights[p - EARLY])
-        return weighed(total, scaled[p - EARLY])
-
-    def take_tables():
-        settle(table_in, table_recv)
-        for k in (1, 2, 3):
-            common, rest = table_in[k - 1, 0:8], table_in[k - 1, 8:16]
-            folded = pltpu.roll(rest, 4, 0)
-            turned = pltpu.roll(common, 4, 0)
-            for p in range(EARLY, prompts):
-                n = p - EARLY
-                gate = jnp.where(rowk < 4, common, rest[n : n + 1])
-                value = jnp.where(rowk < 4, turned, rest[2 + n : 3 + n])
-                set_left(place_of(p, k), p, gate, value, folded)
-
     def send_parts(p):
-        for k in (1, 2, 3):
+        for k in (2, 1, 3):
             peer = lax.rem(m + k, 4)
             pltpu.make_async_remote_copy(
                 src_ref=part.at[p, peer], dst_ref=part_in.at[p, k - 1],
@@ -285,17 +233,6 @@
             lax.fori_loop(1, SCANNERS, step, 0)
             slots_in[p, SLOTS] = drift[p, own_lat, own_half]
 
-    def deliver(p, low, high):
-        def step(peer, carry):
-            pltpu.make_async_remote_copy(
-                src_ref=picked.at[p, peer], dst_ref=whole.at[p, m, own_lat, own_half],
-                send_sem=two_send, recv_sem=two_recv.at[p],
-                device_id={"tm": peer, "mp": m}, device_id_type=MESH,
-            ).start()
-            return carry
-
-        lax.fori_loop(low, high, step, 0)
-
     def scan(p):
         settle(slots_in.at[p, pl.ds(0, SLOTS - 1)], one_recv.at[p])
         slots_in[p, i] = slots_in[p, SLOTS]
@@ -308,37 +245,46 @@
         for j in range(SLOTS):
             picked[p, j] = sums[jnp.minimum(j + by, SLOTS - 1)]
 
-        deliver(p, 0, i)
-        deliver(p, i + 1, NEAR)
+        def deliver(peer, carry):
+            pltpu.make_async_remote_copy(
+                src_ref=picked.at[p, peer], dst_ref=whole.at[p, m, own_lat, own_half],
+                send_sem=two_send, recv_sem=two_recv.at[p],
+                device_id={"tm": peer, "mp": m}, device_id_type=MESH,
+            ).start()
+            return carry
+
+        lax.fori_loop(0, i, deliver, 0)
+        lax.fori_loop(i + 1, SLOTS, deliver, 0)
         whole[p, m, own_lat, own_half] = picked[p, i]
 
     def settle(ref, sem):
         pltpu.make_async_copy(ref, ref, sem).wait()
 
-    for p in range(EARLY):
+    for p in range(prompts):
         for n in range(pos // TILE):
             denoise(p, n)
+        if p == 0:
+
+                @pl.when(scanning)
+                def _():
+                    pl.semaphore_wait(barrier, SCANNERS - 1 + 3)
+
+                @pl.when(resting)
+                def _():
+                    pl.semaphore_wait(barrier, SCANNERS + 3)
+
         send_parts(p)
-    for p in range(EARLY, prompts):
-        denoise_first(p)
-    take_tables()
-    finish(2, denoise_rest(2))
-    finish(0, summed(0))
-    finish(1, summed(1))
-    finish(3, denoise_rest(3))
+        if p == prompts - 1:
+            finish(0, summed(0))
+    for p in range(1, prompts):
+        finish(p, summed(p))
 
     @pl.when(scanning)
     def _():
-        scan(2)
-        deliver(2, NEAR, SLOTS)
-        scan(0)
-        deliver(0, NEAR, SLOTS)
-        scan(1)
-        scan(3)
-        deliver(1, NEAR, SLOTS)
-        deliver(3, NEAR, SLOTS)
-
-    for p in (2, 0, 1, 3):
+        for p in range(prompts):
+            scan(p)
+
+    for p in range(prompts):
 
         @pl.when(scanning)
         def _():
@@ -348,7 +294,7 @@
         def _():
             settle(slots_in.at[p, pl.ds(0, SCANNERS)], two_recv.at[p])
 
-        for k in (1, 2, 3):
+        for k in (2, 1, 3):
             peer = lax.rem(m + k, 4)
             pltpu.make_async_remote_copy(
                 src_ref=whole.at[p, m], dst_ref=whole.at[p, m],
@@ -365,7 +311,6 @@
                 out_ref[p, 0, :, q * share + s * 128 : q * share + (s + 1) * 128] = whole[p, q, :, s // 4, s % 4, :]
 
     settle(part_in, part_send)
-    settle(table_in, table_send)
     settle(whole.at[:, pl.ds(0, 3)], all_send)
 
     @pl.when(scanning)
@@ -407,24 +352,19 @@
         in_specs=[smem, smem] + [vmem] * 7,
         out_specs=(vmem, vmem),
         scratch_shapes=[
-            pltpu.VMEM((EARLY + 4 * (prompts - EARLY), hidden // 16, 16, 128), jnp.bfloat16),
-            pltpu.VMEM((EARLY + 4 * (prompts - EARLY), 64, hidden), jnp.bfloat16),
-            pltpu.VMEM((prompts - EARLY, 128, share), jnp.bfloat16),
-            pltpu.VMEM((prompts - EARLY, 8, share), f32),
-            pltpu.VMEM((prompts - EARLY, 64, share), f32),
-            pltpu.VMEM((16, hidden), f32),
-            pltpu.VMEM((3, 16, hidden), f32),
+            pltpu.VMEM((prompts, hidden // 16, 16, 128), jnp.bfloat16),
+            pltpu.VMEM((prompts, 64, hidden), jnp.bfloat16),
             pltpu.VMEM((8, 8), f32),
             pltpu.VMEM((8, 8), f32),
             pltpu.VMEM((prompts, 3, 8, 128), f32),
-            pltpu.VMEM((EARLY, 4, lats, share), f32),
-            pltpu.VMEM((EARLY, 3, lats, share), f32),
+            pltpu.VMEM((prompts, 4, lats, share), f32),
+            pltpu.VMEM((prompts, 3, lats, share), f32),
             pltpu.VMEM((prompts, lats, 2, 4, 128), f32),
             pltpu.VMEM((prompts, SLOTS + 1, 4, 128), f32),
             pltpu.VMEM((SLOTS, 4, 128), f32),
             pltpu.VMEM((prompts, SLOTS, 4, 128), f32),
             pltpu.VMEM((prompts, 4, lats, 2, 4, 128), f32),
-            dma, dma, dma, dma((EARLY,)), dma, dma((prompts,)), dma, dma((prompts,)), dma, dma((prompts,)),
+            dma, dma((prompts,)), dma, dma((prompts,)), dma, dma((prompts,)), dma, dma((prompts,)),
         ],
         compiler_params=pltpu.CompilerParams(collective_id=0, has_side_effects=True),
         name="sweep",

time: 32.8 us -> 32.7 us (level)
  no operation moved by 1% of the time
where the time goes in v6:
time: 32.7 us; the launch traced here: 32.6 us
  Pallas kernels  32 us (98%)
  between operations  0.64 us (2%)
    pallas_call x1, Pallas kernels, shards(): pl.pallas_call(sweep, out_shape=(pltpu.VMEM(latents.shape, f32), pltpu.VM...  31.3 us
    pallas_call x1, Pallas kernels, shards(): pl.pallas_call(put_out, out_shape=(jax.ShapeDtypeStruct(latents.shape, f3...  0.74 us

profile of v6, /device:TPU:1, one launch (start us, length us, event | category | flops | bytes accessed | tf_op | source)
XLA Modules:
  0.0 32.6 jit_solution(5408933881609028759)
XLA Ops:
  0.6 31.3 %sweep.1 = (f32[4,1,4,4096]{3,2,1,0:T(4,128)S(1)}, f32[4,1,4,1024]{3,2,1,0:T(4,128)S(1)}) custom-call(s32[4]{0:T(128)} %start.1, s32[4]{0:T(128)} %slide.1, f32[4,1,4,4096]{3,2,1,0:T(4,128)} %lat_ref.1, f32[4,1,4,4096]{3,2,1,0:T(4,128)} %noise_ref.1, f32[4,320]{1,0:T(4,128)} %w_in_ref.1, bf16[320,320]{1,0:T(8,128)(2,1)} %w_gate_ref.1, ...), custom_call_target="tpu_custom_call" | custom-call | tf_op jit(solution)/shard_map/sweep/pallas_call | solution.py:346
  31.9 0.7 %put_out.1 = (f32[4,1,4,4096]{3,2,1,0:T(4,128)}, f32[4,1,4,1024]{3,2,1,0:T(4,128)}) custom-call(f32[4,1,4,4096]{3,2,1,0:T(4,128)S(1)} %get-tuple-element.4.window, f32[4,1,4,1024]{3,2,1,0:T(4,128)S(1)} %get-tuple-element.5.eps), custom_call_target="tpu_custom_call" | custom-call | tf_op jit(solution)/shard_map/put_out/pallas_call | solution.py:372

commit v7 on v6

--- a/solution.py
+++ b/solution.py
@@ -153,7 +153,7 @@
         for b in range(4):
             z = z + cov[:, b : b + 1] * x4[b : b + 1, :]
         var = jnp.sum(x * z, axis=0, keepdims=True) + cov[4 + p : 5 + p, 4 + p : 5 + p]
-        scale = lax.rsqrt(var + 1e-05)
+        scale = lax.rsqrt(jnp.maximum(var, 0.0) + 1e-05)
         y = jnp.where(rowt < 4, x8, jnp.where(rowt == 4, 1.0, 0.0)) * scale
         high, mid, low = split3(y)
         right = jnp.concatenate(

time: 32.7 us -> 32.8 us (level)
  no operation moved by 1% of the time
where the time goes in v7:
time: 32.8 us; the launch traced here: 32.7 us
  Pallas kernels  32 us (98%)
  between operations  0.64 us (2%)
    pallas_call x1, Pallas kernels, shards(): pl.pallas_call(sweep, out_shape=(pltpu.VMEM(latents.shape, f32), pltpu.VM...  31.3 us
    pallas_call x1, Pallas kernels, shards(): pl.pallas_call(put_out, out_shape=(jax.ShapeDtypeStruct(latents.shape, f3...  0.74 us

profile of v7, /device:TPU:1, one launch (start us, length us, event | category | flops | bytes accessed | tf_op | source)
XLA Modules:
  0.0 32.7 jit_solution(15448445458844507241)
XLA Ops:
  0.6 31.3 %sweep.1 = (f32[4,1,4,4096]{3,2,1,0:T(4,128)S(1)}, f32[4,1,4,1024]{3,2,1,0:T(4,128)S(1)}) custom-call(s32[4]{0:T(128)} %start.1, s32[4]{0:T(128)} %slide.1, f32[4,1,4,4096]{3,2,1,0:T(4,128)} %lat_ref.1, f32[4,1,4,4096]{3,2,1,0:T(4,128)} %noise_ref.1, f32[4,320]{1,0:T(4,128)} %w_in_ref.1, bf16[320,320]{1,0:T(8,128)(2,1)} %w_gate_ref.1, ...), custom_call_target="tpu_custom_call" | custom-call | tf_op jit(solution)/shard_map/sweep/pallas_call | solution.py:346
  31.9 0.7 %put_out.1 = (f32[4,1,4,4096]{3,2,1,0:T(4,128)}, f32[4,1,4,1024]{3,2,1,0:T(4,128)}) custom-call(f32[4,1,4,4096]{3,2,1,0:T(4,128)S(1)} %get-tuple-element.4.window, f32[4,1,4,1024]{3,2,1,0:T(4,128)S(1)} %get-tuple-element.5.eps), custom_call_target="tpu_custom_call" | custom-call | tf_op jit(solution)/shard_map/put_out/pallas_call | solution.py:372
